TPU v7x, 32 devices: a whole 2x2x4 slice. The times are simulated.
32 devices in a mesh: dp: 2 (over x), tp2: 4 (over z), tp: 4 (over y, core).
Axes of the slice: x: 2, y: 2, z: 4, core: 2. Of those that a mesh axis runs over, the one named last changes fastest.
Arguments:
- attn_out: bfloat16 [16384, 8192], P('dp', 'tp'), parts along dimension 0
- w_out: bfloat16 [8192, 8192], P('tp', 'tp2')
- residual: bfloat16 [16384, 8192], P(('dp', 'tp'), 'tp2'), parts along dimension 0
- norm_gain: float32 [8192], P('tp2')
Outputs:
- output 1: bfloat16 [16384, 8192], P(('dp', 'tp'), 'tp2'), parts along dimension 0
- output 2: bfloat16 [16384, 8192], P(('dp', 'tp'), 'tp2'), parts along dimension 0
There are 2 independent parts. A program takes and returns all parts, laid end to end along the dimension named above; an argument that names none is the same for every part.
All inputs are finite; a program needn't handle non-finite values.
Results may differ from a plain program's by a relative error of at most 0.00720324.
Values are sent between devices in bfloat16 or wider.
A program may use at most 1 GiB of HBM per device.

v0:
```python
import jax
import jax.numpy as jnp
from jax import lax
from jax.sharding import PartitionSpec as P, NamedSharding

EPS_NORM = 1e-6


def solution(mesh):
    tp_size = mesh.shape["tp"]
    col_groups = mesh.shape["tp2"]

    def local_step(attn_blk, w_blk, res_blk, gain_blk):
        block_prod = jnp.dot(attn_blk, w_blk, preferred_element_type=jnp.float32).astype(jnp.bfloat16)
        token_rows, local_cols = block_prod.shape
        received = lax.all_to_all(block_prod, "tp", 0, 0, tiled=True)
        y_sum = jnp.sum(received.reshape(tp_size, token_rows // tp_size, local_cols), axis=0, dtype=jnp.float32)
        hidden = res_blk.astype(jnp.float32) + y_sum
        sq_sum = lax.psum(jnp.sum(hidden * hidden, axis=-1, keepdims=True), "tp2")
        inv_rms = lax.rsqrt(sq_sum / (local_cols * col_groups) + EPS_NORM)
        normed = hidden * inv_rms * gain_blk
        return hidden.astype(jnp.bfloat16), normed.astype(jnp.bfloat16)

    row_spec = P(("dp", "tp"), "tp2")
    return jax.shard_map(local_step, mesh=mesh, in_specs=(P("dp", "tp"), P("tp", "tp2"), row_spec, P("tp2")), out_specs=(row_spec, row_spec), check_vma=False)
```

profile of v0, /device:TPU:0, one launch (start us, length us, event | category | flops | bytes accessed | tf_op | source)
XLA Modules:
  0.0 514.9 jit_solution(8163568783573321929)
XLA Ops:
  0.6 77.2 %convolution_convert_fusion = bf16[8192,2048]{1,0:T(8,128)(2,1)} fusion(bf16[8192,2048]{1,0:T(8,128)(2,1)} %param.4, bf16[2048,2048]{1,0:T(8,128)(2,1)} %param.5), kind=kOutput, calls=%fused_computation.1 | convolution fusion | flops 68736253952 | bytes 75497472 | tf_op jit(solution)/shard_map/dot_general | solution.py:14
  77.8 381.4 %all_to_all.9 = bf16[4,2048,2048]{2,1,0:T(8,128)(2,1)} all-to-all(bf16[4,2048,2048]{2,1,0:T(8,128)(2,1)} %bitcast.5), channel_id=1, replica_groups=mesh['dp'=2,'tp2'=4,'tp'=4] {'tp'}, dimensions={0} | all-to-all | bytes 67108864 | tf_op jit(solution)/shard_map/all_to_all | solution.py:16
  459.2 0.0 copy-start.1
  459.2 19.4 %convert_reduce_fusion = f32[2048,2048]{1,0:T(8,128)S(1)} fusion(bf16[4,2048,2048]{2,1,0:T(8,128)(2,1)} %all_to_all.9), kind=kLoop, calls=%fused_computation | loop fusion | flops 29360128 | bytes 50331648 | tf_op jit(solution)/shard_map/reduce_sum | solution.py:17
  478.7 0.0 copy-start
  478.7 5.7 %copy-done = f32[2048,2048]{1,0:T(8,128)} copy-done((f32[2048,2048]{1,0:T(8,128)}, f32[2048,2048]{1,0:T(8,128)S(1)}, u32[]{:S(2)}) %copy-start) | copy-done | bytes 16777240
  484.4 0.0 copy-done.1
  484.4 0.0 copy-start.2
  484.4 2.5 multiply_reduce_fusion
  486.9 12.9 %psum.7 = f32[2048,1]{0,1:T(1,128)S(1)} all-reduce(f32[2048,1]{0,1:T(1,128)S(1)} %bitcast.7), channel_id=1, replica_groups=mesh['dp'=2,'tp2'=4,'tp'=4] {'tp2'}, use_global_device_ids=true, to_apply=%region_2.0 | all-reduce | flops 2048 | bytes 16384 | tf_op jit(solution)/shard_map/psum | solution.py:19
  499.8 0.0 copy-done.2
  499.8 15.1 %multiply_convert_fusion = (bf16[2048,2048]{1,0:T(8,128)(2,1)}, bf16[2048,2048]{1,0:T(8,128)(2,1)}) fusion(f32[2048]{0:T(1024)S(1)} %copy-done.2, f32[2048]{0:T(1024)S(1)} %bitcast.6, f32[2048,2048]{1,0:T(8,128)} %copy-done, bf16[2048,2048]{1,0:T(8,128)(2,1)} %param.6), kind=kLoop, calls=%fused_computation.2 | loop fusion | flops 25165824 | bytes 41959424 | tf_op jit(solution)/shard_map/convert_element_type | solution.py:22
  (1 shorter events, 0.0 us)
Async XLA Ops:
  459.2 25.2 %copy-start.1 = (bf16[2048,2048]{1,0:T(8,128)(2,1)S(1)}, bf16[2048,2048]{1,0:T(8,128)(2,1)}, u32[]{:S(2)}) copy-start(bf16[2048,2048]{1,0:T(8,128)(2,1)} %param.6) | copy-start | bytes 25165828
  478.7 5.7 %copy-start = (f32[2048,2048]{1,0:T(8,128)}, f32[2048,2048]{1,0:T(8,128)S(1)}, u32[]{:S(2)}) copy-start(f32[2048,2048]{1,0:T(8,128)S(1)} %convert_reduce_fusion) | copy-start | bytes 50331652
  484.4 15.4 %copy-start.2 = (f32[2048]{0:T(1024)S(1)}, f32[2048]{0:T(1024)}, u32[]{:S(2)}) copy-start(f32[2048]{0:T(1024)} %param.7) | copy-start | bytes 24580
where the time goes:
time: 516 us; the launch traced here: 515 us
  blocking collectives  394 us (76%)
  matrix products  77.2 us (15%)
  other arithmetic  37.1 us (7%)
  local copies, waits for them, and re-layouts  5.71 us (1%)
    all_to_all x1, blocking collectives, local_step(): received = lax.all_to_all(block_prod, 'tp', 0, 0, tiled=True)  381 us
    dot_general x1, matrix products, local_step(): jnp.dot(attn_blk, w_blk, preferred_element_type=jnp.float32)  77.2 us
    reduce_sum x1, other arithmetic, local_step(): jnp.sum(received.reshape(tp_size, token_rows // tp_size, local_cols), axi...  19.4 us
    convert_element_type x1, other arithmetic, local_step(): return (hidden.astype(jnp.bfloat16), normed.astype(jnp.bfloat16))  15.1 us
    psum x1, blocking collectives, local_step(): sq_sum = lax.psum(jnp.sum(hidden * hidden, axis=-1, keepdims=True), 'tp2')  12.9 us

commit v1 on v0

v1 whole, which is shorter than its diff:
```python
import functools

import jax
import jax.numpy as jnp
from jax import lax
from jax.experimental import pallas as pl
from jax.experimental.pallas import tpu as pltpu
from jax.sharding import PartitionSpec as P

EPS_NORM = 1e-6
MESH = pl.DeviceIdType.MESH
NCH = 32
NWC = 8
GRP = 4
NUNIT = NCH // GRP
AHEAD = 3
NSLOT = 21
LOCAL0 = 2


def step_count(i, slots):
    n = jnp.int32(0)
    for s in slots:
        n = n + jnp.where(i >= s, 1, 0)
    return n


END_UNITS = (10, 10, 12, 13, 16, 17, 19, 20)
MID_UNITS = (17, 18, 19, 19, 19, 20, 20, 20)


def kernel(a, w, r, g, h_out, n_out, ax, ap, wl, wr, acc, abuf, rbuf, obuf, ss_loc, ss_all,
           recv_a, send_ya, send_yw, send_zi, send_zo, recv_wy, recv_wx, recv_wd, send_wx, send_wd,
           recv_da, recv_dw, send_da, send_dw, load_sem, load_w, out_sem, send_ss, recv_ss):
    x = lax.axis_index("dp")
    z = lax.axis_index("tp2")
    t = lax.axis_index("tp")
    y = t // 2
    c = t % 2
    rows, cols = acc.shape
    kb = w.shape[0]
    ch = rows // NCH
    wch = kb // 2 // NWC
    unit = ch * GRP
    side = z // 2
    end = (z == 0) | (z == 3)
    mid = (z == 1) | (z == 2)
    base = side * (NCH // 2)
    other = (1 - side) * (NCH // 2)
    z_in = jnp.where(side == 0, z + 1, z - 1)
    z_out = jnp.where(side == 0, z - 1, z + 1)

    partner = (x, z, y * 2 + 1 - c)
    x_peer = (1 - x, z, t)
    y_same = (x, z, (1 - y) * 2 + c)
    y_cross = (x, z, (1 - y) * 2 + 1 - c)

    def remote(src, dst, send, recv, dev):
        return pltpu.make_async_remote_copy(
            src_ref=src, dst_ref=dst, send_sem=send, recv_sem=recv, device_id=dev, device_id_type=MESH)

    def wait_bytes(ref, sem):
        pltpu.make_async_copy(ref, ref, sem).wait()

    barrier = pltpu.get_barrier_semaphore()
    for dev in (partner, x_peer, y_same, y_cross):
        pl.semaphore_signal(barrier, inc=1, device_id=dev, device_id_type=MESH)
    for k in range(1, 4):
        pl.semaphore_signal(barrier, inc=1, device_id=(x, lax.rem(z + k, 4), t), device_id_type=MESH)
    pl.semaphore_wait(barrier, 7)

    def mp(start, j):
        return start + NCH // 4 + lax.rem(j + NCH // 8, NCH // 4)

    def send_y_a(q):
        for cc in range(2):
            row = ((1 - y) * 2 + cc) * rows + q * ch
            remote(a.at[pl.ds(pl.multiple_of(row, ch), ch)], ax.at[q, c], send_ya, recv_a.at[q],
                   (x, z, (1 - y) * 2 + cc)).start()

    def w_rows(half, i):
        return pl.ds(pl.multiple_of(half * (kb // 2) + i * wch, wch), wch)

    def send_y_w(i):
        remote(w.at[w_rows(x, i)], wr.at[c, w_rows(x, i)], send_yw, recv_wy.at[i], y_same).start()

    def y_sends(i):
        @pl.when(end & (i < NWC))
        def _():
            send_y_w(i)

        @pl.when(end & (i >= NWC) & (i < NWC + 12))
        def _():
            send_y_a(base + i - NWC)

        @pl.when(mid & (i < 8))
        def _():
            send_y_a(mp(base, i))

        @pl.when(mid & (i >= 8) & (i < 8 + NWC))
        def _():
            send_y_w(i - 8)

    lax.fori_loop(0, AHEAD, lambda i, _: (y_sends(i), None)[1], None)

    remote(w, wl.at[1], send_dw, recv_dw, partner).start()
    prow = pl.ds(pl.multiple_of((y * 2 + 1 - c) * rows, rows), rows)
    remote(a.at[prow], ap, send_da, recv_da, partner).start()
    own_w = pltpu.make_async_copy(w, wl.at[0], load_w)
    own_w.start()

    def arrive(q):
        wait_bytes(ax.at[q], recv_a.at[q])

    def pass_in(q):
        remote(ax.at[q], ax.at[q], send_zi, recv_a.at[q], (x, z_in, t)).start()

    def pass_out(q):
        remote(ax.at[q], ax.at[q], send_zo, recv_a.at[q], (x, z_out, t)).start()

    def w_from_y(i):
        part = wr.at[c, w_rows(x, i)]
        wait_bytes(part, recv_wy.at[i])
        remote(part, part, send_wx, recv_wx.at[i], x_peer).start()
        remote(part, part, send_wd, recv_wd, partner).start()

    def w_from_x(i):
        part = wr.at[c, w_rows(1 - x, i)]
        wait_bytes(part, recv_wx.at[i])
        remote(part, part, send_wd, recv_wd, partner).start()

    def comm(i):
        y_sends(i + AHEAD)

        @pl.when(end)
        def _():
            @pl.when(i < NWC)
            def _():
                w_from_y(i)

            @pl.when((i >= NWC) & (i < NWC + 12))
            def _():
                q = base + i - NWC
                arrive(q)

                @pl.when(i < NWC + 8)
                def _():
                    pass_in(q)

            @pl.when((i >= 1) & (i < 1 + NWC))
            def _():
                w_from_x(i - 1)

            j = i - 1

            @pl.when((j >= 0) & (j < 4))
            def _():
                arrive(mp(base, j))

            @pl.when((j >= 4) & (j < 12))
            def _():
                arrive(mp(other, j - 4))

            @pl.when((j >= 12) & (j < 20))
            def _():
                arrive(other + j - 12)

        @pl.when(mid)
        def _():
            @pl.when(i < 8)
            def _():
                q = mp(base, i)
                arrive(q)

                @pl.when(i < 4)
                def _():
                    pass_out(q)

                pass_in(q)

            @pl.when((i >= 1) & (i < 9))
            def _():
                q = mp(other, i - 1)
                arrive(q)
                pass_out(q)

            @pl.when((i >= 9) & (i < 17))
            def _():
                q = base + i - 9
                arrive(q)
                pass_in(q)

            @pl.when((i >= 10) & (i < 18))
            def _():
                q = other + i - 10
                arrive(q)
                pass_out(q)

            @pl.when((i >= 8) & (i < 8 + NWC))
            def _():
                w_from_y(i - 8)

            @pl.when((i >= 9) & (i < 9 + NWC))
            def _():
                w_from_x(i - 9)

    tn = min(512, cols)
    ntile = cols // tn

    def local_loads(u):
        slot = lax.rem(u, 2)
        here = pl.ds(pl.multiple_of(u * unit, unit), unit)
        mine = pl.ds(pl.multiple_of(t * rows + u * unit, unit), unit)
        return (pltpu.make_async_copy(a.at[mine], abuf.at[slot, 0], load_sem.at[slot, 0]),
                pltpu.make_async_copy(ap.at[here], abuf.at[slot, 1], load_sem.at[slot, 1]),
                pltpu.make_async_copy(r.at[here], rbuf.at[slot], load_sem.at[slot, 2]))

    def local_unit(u):
        slot = lax.rem(u, 2)
        here = pl.ds(pl.multiple_of(u * unit, unit), unit)
        for cp in local_loads(u):
            cp.wait()

        @pl.when(u + 1 < NUNIT)
        def _():
            for cp in local_loads(u + 1):
                cp.start()

        def tile(n, _):
            cs = pl.ds(pl.multiple_of(n * tn, tn), tn)
            p0 = jnp.dot(abuf[slot, 0], wl[0, :, cs], preferred_element_type=jnp.float32)
            p1 = jnp.dot(abuf[slot, 1], wl[1, :, cs], preferred_element_type=jnp.float32)
            acc[here, cs] = (rbuf[slot, :, cs].astype(jnp.float32) + p0.astype(jnp.bfloat16).astype(jnp.float32)
                             + p1.astype(jnp.bfloat16).astype(jnp.float32))
            return None

        lax.fori_loop(0, ntile, tile, None)

    def out_copy(u, q, dst, k):
        here = pl.ds(pl.multiple_of(q * unit, unit), unit)
        return pltpu.make_async_copy(obuf.at[lax.rem(u, 2)], dst.at[here], out_sem.at[lax.rem(u, 2)])

    def unit_of(u):
        gs = NUNIT // 2
        b = side * gs
        o = (1 - side) * gs
        end_order = (b + 3, o + 3, b, o + 2, b + 1, o, b + 2, o + 1)
        mid_order = (b + 3, b + 2, o + 3, o + 2, b, o, b + 1, o + 1)
        q = jnp.int32(0)
        for k in range(NUNIT):
            q = q + jnp.where(u == k, jnp.where(end, end_order[k], mid_order[k]), 0)
        return q

    def remote_unit(u, _):
        q = unit_of(u)
        here = pl.ds(pl.multiple_of(q * unit, unit), unit)
        slot = lax.rem(u, 2)
        loads = [pltpu.make_async_copy(ax.at[pl.ds(q * GRP, GRP), b], abuf.at[slot, b].reshape(GRP, ch, kb),
                                       load_sem.at[slot, b]) for b in range(2)]
        for cp in loads:
            cp.start()

        @pl.when(u >= 2)
        def _():
            out_copy(u, q, h_out, 0).wait()

        for cp in loads:
            cp.wait()

        def tile(n, part):
            cs = pl.ds(pl.multiple_of(n * tn, tn), tn)
            p0 = jnp.dot(abuf[slot, 0], wr[0, :, cs], preferred_element_type=jnp.float32)
            p1 = jnp.dot(abuf[slot, 1], wr[1, :, cs], preferred_element_type=jnp.float32)
            v = acc[here, cs] + (p0.astype(jnp.bfloat16).astype(jnp.float32) + p1.astype(jnp.bfloat16).astype(jnp.float32))
            acc[here, cs] = v
            obuf[slot, :, cs] = v.astype(jnp.bfloat16)
            sq = v * v
            for k in range(tn // 128):
                part = part + sq[:, k * 128:(k + 1) * 128]
            return part

        part = lax.fori_loop(0, ntile, tile, jnp.zeros((unit, 128), jnp.float32))
        out_copy(u, q, h_out, 0).start()
        for k in range(unit // 128):
            ss_loc[q, k:k + 1, :] = jnp.sum(part[k * 128:(k + 1) * 128, :].T, axis=0, keepdims=True)
        return None

    def slot_body(i, _):
        comm(i)

        @pl.when(i == LOCAL0 - 1)
        def _():
            own_w.wait()
            wait_bytes(wl.at[1], recv_dw)
            wait_bytes(ap, recv_da)
            for cp in local_loads(0):
                cp.start()

        @pl.when((i >= LOCAL0) & (i < LOCAL0 + NUNIT))
        def _():
            local_unit(i - LOCAL0)

        @pl.when(i == jnp.where(end, END_UNITS[0], MID_UNITS[0]))
        def _():
            wait_bytes(wr.at[1 - c], recv_wd)

        lo = jnp.where(end, step_count(i - 1, END_UNITS), step_count(i - 1, MID_UNITS))
        hi = jnp.where(end, step_count(i, END_UNITS), step_count(i, MID_UNITS))
        lax.fori_loop(lo, hi, remote_unit, None)
        return None

    lax.fori_loop(0, NSLOT, slot_body, None)

    for k in range(1, 4):
        remote(ss_loc, ss_all.at[z], send_ss.at[k - 1], recv_ss.at[z], (x, lax.rem(z + k, 4), t)).start()
    for u in range(NUNIT - 2, NUNIT):
        out_copy(jnp.int32(u), jnp.int32(0), h_out, 0).wait()
    wait_bytes(wl.at[1], send_dw)
    wait_bytes(ap, send_da)
    wait_bytes(wr.at[0], send_wd)
    wait_bytes(wr.at[0, pl.ds(0, kb // 2)], send_wx)
    wait_bytes(wr.at[0, pl.ds(0, kb // 2)], send_yw)

    @pl.when(end)
    def _():
        wait_bytes(ax.at[pl.ds(0, 12)], send_ya)
        wait_bytes(ax.at[pl.ds(0, 8)], send_zi)

    @pl.when(mid)
    def _():
        wait_bytes(ax.at[pl.ds(0, 8)], send_ya)
        wait_bytes(ax.at[pl.ds(0, 16)], send_zi)
        wait_bytes(ax.at[pl.ds(0, 20)], send_zo)

    for k in range(1, 4):
        src = lax.rem(z + k, 4)
        remote(ss_loc, ss_all.at[src], send_ss.at[k - 1], recv_ss.at[src], (x, src, t)).wait_recv()
        remote(ss_loc, ss_all.at[src], send_ss.at[k - 1], recv_ss.at[src], (x, src, t)).wait_send()
    ss_all[z] = ss_loc[...]

    def finish(q, _):
        here = pl.ds(pl.multiple_of(q * unit, unit), unit)
        slot = lax.rem(q, 2)

        @pl.when(q >= 2)
        def _():
            out_copy(q, q, n_out, 1).wait()

        total = ss_all[0, q] + ss_all[1, q] + ss_all[2, q] + ss_all[3, q]
        inv = lax.rsqrt(total / (cols * 4) + EPS_NORM)
        for k in range(unit // 128):
            col = jnp.broadcast_to(inv[k:k + 1, :], (128, 128)).T
            rs = pl.ds(pl.multiple_of(q * unit + k * 128, 128), 128)
            for m in range(cols // 128):
                cs = slice(m * 128, (m + 1) * 128)
                obuf[slot, k * 128:(k + 1) * 128, cs] = (acc[rs, cs] * col * g[:, cs]).astype(jnp.bfloat16)
        out_copy(q, q, n_out, 1).start()
        return None

    lax.fori_loop(0, NUNIT, finish, None)
    for u in range(NUNIT - 2, NUNIT):
        out_copy(jnp.int32(u), jnp.int32(0), n_out, 1).wait()


def solution(mesh):
    def local_step(attn_blk, w_blk, res_blk, gain_blk):
        kb = attn_blk.shape[1]
        rows, cols = res_blk.shape
        unit = rows // NUNIT
        any_spec = pl.BlockSpec(memory_space=pl.ANY)
        bf16, f32 = jnp.bfloat16, jnp.float32
        dma = pltpu.SemaphoreType.DMA
        outs = pl.pallas_call(
            kernel,
            out_shape=(
                jax.ShapeDtypeStruct((rows, cols), bf16),
                jax.ShapeDtypeStruct((rows, cols), bf16),
                jax.ShapeDtypeStruct((NCH, 2, rows // NCH, kb), bf16),
                jax.ShapeDtypeStruct((rows, kb), bf16),
            ),
            in_specs=[any_spec, any_spec, any_spec, pl.BlockSpec(memory_space=pltpu.VMEM)],
            out_specs=(any_spec,) * 4,
            scratch_shapes=[
                pltpu.VMEM((2, kb, cols), bf16),
                pltpu.VMEM((2, kb, cols), bf16),
                pltpu.VMEM((rows, cols), f32),
                pltpu.VMEM((2, 2, unit, kb), bf16),
                pltpu.VMEM((2, unit, cols), bf16),
                pltpu.VMEM((2, unit, cols), bf16),
                pltpu.VMEM((NUNIT, unit // 128, 128), f32),
                pltpu.VMEM((4, NUNIT, unit // 128, 128), f32),
                dma((NCH,)), dma, dma, dma, dma,
                dma((NWC,)), dma((NWC,)), dma, dma, dma,
                dma, dma, dma, dma,
                dma((2, 3)), dma, dma((2,)),
                dma((3,)), dma((4,)),
            ],
            compiler_params=pltpu.CompilerParams(
                collective_id=0, has_side_effects=True, vmem_limit_bytes=64 * 1024 * 1024 - 65536),
            name="gather_project_norm",
        )(attn_blk, w_blk, res_blk, gain_blk.reshape(1, cols))
        return outs[0], outs[1]

    row_spec = P(("dp", "tp"), "tp2")
    return jax.shard_map(local_step, mesh=mesh, in_specs=(P("dp", "tp"), P("tp", "tp2"), row_spec, P("tp2")), out_specs=(row_spec, row_spec), check_vma=False)
```

time: 516 us -> 301 us (0.58)
  blocking collectives: 394 us -> 0 us
  Pallas kernels: 0 us -> 280 us
  matrix products: 77.2 us -> 0 us
  other arithmetic: 37.1 us -> 0 us
  local copies, waits for them, and re-layouts: 5.71 us -> 16.9 us
    all_to_all x1 -> x0, blocking collectives: 381 us -> none  [local_step(): received = lax.all_to_all(block_prod, 'tp', 0, 0, tiled=True)]
    pallas_call x0 -> x1, Pallas kernels: none -> 280 us  [local_step(): pl.pallas_call(kernel, out_shape=(jax.ShapeDtypeStruct((rows, cols), bf16...]
    dot_general x1 -> x0, matrix products: 77.2 us -> none  [local_step(): jnp.dot(attn_blk, w_blk, preferred_element_type=jnp.float32)]
    reduce_sum x2 -> x0, other arithmetic: 21.9 us -> none  [the longest x1 19.4 us: local_step(): jnp.sum(received.reshape(tp_size, token_rows // tp_size, local_cols), axi...]
    convert_element_type x1 -> x0, other arithmetic: 15.1 us -> none  [local_step(): return (hidden.astype(jnp.bfloat16), normed.astype(jnp.bfloat16))]
    psum x1 -> x0, blocking collectives: 12.9 us -> none  [local_step(): sq_sum = lax.psum(jnp.sum(hidden * hidden, axis=-1, keepdims=True), 'tp2')]
    unnamed x6 -> x2, local copies, waits for them, and re-layouts: 5.71 us -> 16.9 us
where the time goes in v1:
time: 301 us; the launch traced here: 298 us
  Pallas kernels  280 us (93%)
  local copies, waits for them, and re-layouts  16.9 us (6%)
    pallas_call x1, Pallas kernels, local_step(): pl.pallas_call(kernel, out_shape=(jax.ShapeDtypeStruct((rows, cols), bf16...  280 us
    unnamed x2, local copies, waits for them, and re-layouts  16.9 us

profile of v1, /device:TPU:0, one launch (start us, length us, event | category | flops | bytes accessed | tf_op | source)
XLA Modules:
  0.0 298.0 jit_solution(5857811268927697360)
XLA Ops:
  0.6 280.5 %gather_project_norm.1 = (bf16[2048,2048]{1,0:T(8,128)(2,1)}, bf16[2048,2048]{1,0:T(8,128)(2,1)}, bf16[32,2,64,2048]{3,2,1,0:T(8,128)(2,1)}, bf16[2048,2048]{1,0:T(8,128)(2,1)}) custom-call(bf16[8192,2048]{1,0:T(8,128)(2,1)} %a.1, bf16[2048,2048]{1,0:T(8,128)(2,1)} %w.1, bf16[2048,2048]{1,0:T(8,128)(2,1)} %r.1, f32[1,2048]{1,0:T(1,128)} %bitcast.1), custom_call_target="tpu_custom_call" | custom-call | tf_op jit(solution)/shard_map/gather_project_norm/pallas_call | solution.py:373
  281.1 8.4 %copy.8 = bf16[2048,2048]{1,0:T(8,128)(2,1)} copy(bf16[2048,2048]{1,0:T(8,128)(2,1)} %get-tuple-element.8) | data formatting | bytes 16777216
  289.6 8.4 %copy.9 = bf16[2048,2048]{1,0:T(8,128)(2,1)} copy(bf16[2048,2048]{1,0:T(8,128)(2,1)} %get-tuple-element.9) | data formatting | bytes 16777216

commit v2 on v1

--- a/solution.py
+++ b/solution.py
@@ -29,9 +29,9 @@
 MID_UNITS = (17, 18, 19, 19, 19, 20, 20, 20)
 
 
-def kernel(a, w, r, g, h_out, n_out, ax, ap, wl, wr, acc, abuf, rbuf, obuf, ss_loc, ss_all,
+def kernel(a, w, r, acc, ss_all, ax, ap, wl, wr, abuf, rbuf, ss_loc,
            recv_a, send_ya, send_yw, send_zi, send_zo, recv_wy, recv_wx, recv_wd, send_wx, send_wd,
-           recv_da, recv_dw, send_da, send_dw, load_sem, load_w, out_sem, send_ss, recv_ss):
+           recv_da, recv_dw, send_da, send_dw, load_sem, load_w, send_ss, recv_ss):
     x = lax.axis_index("dp")
     z = lax.axis_index("tp2")
     t = lax.axis_index("tp")
@@ -236,10 +236,6 @@
 
         lax.fori_loop(0, ntile, tile, None)
 
-    def out_copy(u, q, dst, k):
-        here = pl.ds(pl.multiple_of(q * unit, unit), unit)
-        return pltpu.make_async_copy(obuf.at[lax.rem(u, 2)], dst.at[here], out_sem.at[lax.rem(u, 2)])
-
     def unit_of(u):
         gs = NUNIT // 2
         b = side * gs
@@ -260,10 +256,6 @@
         for cp in loads:
             cp.start()
 
-        @pl.when(u >= 2)
-        def _():
-            out_copy(u, q, h_out, 0).wait()
-
         for cp in loads:
             cp.wait()
 
@@ -273,14 +265,12 @@
             p1 = jnp.dot(abuf[slot, 1], wr[1, :, cs], preferred_element_type=jnp.float32)
             v = acc[here, cs] + (p0.astype(jnp.bfloat16).astype(jnp.float32) + p1.astype(jnp.bfloat16).astype(jnp.float32))
             acc[here, cs] = v
-            obuf[slot, :, cs] = v.astype(jnp.bfloat16)
             sq = v * v
             for k in range(tn // 128):
                 part = part + sq[:, k * 128:(k + 1) * 128]
             return part
 
         part = lax.fori_loop(0, ntile, tile, jnp.zeros((unit, 128), jnp.float32))
-        out_copy(u, q, h_out, 0).start()
         for k in range(unit // 128):
             ss_loc[q, k:k + 1, :] = jnp.sum(part[k * 128:(k + 1) * 128, :].T, axis=0, keepdims=True)
         return None
@@ -313,8 +303,6 @@
 
     for k in range(1, 4):
         remote(ss_loc, ss_all.at[z], send_ss.at[k - 1], recv_ss.at[z], (x, lax.rem(z + k, 4), t)).start()
-    for u in range(NUNIT - 2, NUNIT):
-        out_copy(jnp.int32(u), jnp.int32(0), h_out, 0).wait()
     wait_bytes(wl.at[1], send_dw)
     wait_bytes(ap, send_da)
     wait_bytes(wr.at[0], send_wd)
@@ -338,28 +326,43 @@
         remote(ss_loc, ss_all.at[src], send_ss.at[k - 1], recv_ss.at[src], (x, src, t)).wait_send()
     ss_all[z] = ss_loc[...]
 
-    def finish(q, _):
+def finish_kernel(h, ss, g, h_out, n_out, hbuf, nbuf, sem):
+    rows, cols = h.shape
+    unit = rows // NUNIT
+    nfin = NUNIT
+
+    def copies(q):
+        slot = lax.rem(q, 2)
         here = pl.ds(pl.multiple_of(q * unit, unit), unit)
+        return (pltpu.make_async_copy(hbuf.at[slot], h_out.at[here], sem.at[slot, 0]),
+                pltpu.make_async_copy(nbuf.at[slot], n_out.at[here], sem.at[slot, 1]))
+
+    def step(q, _):
         slot = lax.rem(q, 2)
 
         @pl.when(q >= 2)
         def _():
-            out_copy(q, q, n_out, 1).wait()
-
-        total = ss_all[0, q] + ss_all[1, q] + ss_all[2, q] + ss_all[3, q]
+            for cp in copies(q - 2):
+                cp.wait()
+
+        total = ss[0, q] + ss[1, q] + ss[2, q] + ss[3, q]
         inv = lax.rsqrt(total / (cols * 4) + EPS_NORM)
         for k in range(unit // 128):
             col = jnp.broadcast_to(inv[k:k + 1, :], (128, 128)).T
             rs = pl.ds(pl.multiple_of(q * unit + k * 128, 128), 128)
             for m in range(cols // 128):
                 cs = slice(m * 128, (m + 1) * 128)
-                obuf[slot, k * 128:(k + 1) * 128, cs] = (acc[rs, cs] * col * g[:, cs]).astype(jnp.bfloat16)
-        out_copy(q, q, n_out, 1).start()
+                v = h[rs, cs]
+                hbuf[slot, k * 128:(k + 1) * 128, cs] = v.astype(jnp.bfloat16)
+                nbuf[slot, k * 128:(k + 1) * 128, cs] = (v * col * g[:, cs]).astype(jnp.bfloat16)
+        for cp in copies(q):
+            cp.start()
         return None
 
-    lax.fori_loop(0, NUNIT, finish, None)
-    for u in range(NUNIT - 2, NUNIT):
-        out_copy(jnp.int32(u), jnp.int32(0), n_out, 1).wait()
+    lax.fori_loop(0, nfin, step, None)
+    for q in (nfin - 2, nfin - 1):
+        for cp in copies(jnp.int32(q)):
+            cp.wait()
 
 
 def solution(mesh):
@@ -368,38 +371,44 @@
         rows, cols = res_blk.shape
         unit = rows // NUNIT
         any_spec = pl.BlockSpec(memory_space=pl.ANY)
+        vmem_spec = pl.BlockSpec(memory_space=pltpu.VMEM)
         bf16, f32 = jnp.bfloat16, jnp.float32
         dma = pltpu.SemaphoreType.DMA
-        outs = pl.pallas_call(
+        h, ss, _, _ = pl.pallas_call(
             kernel,
             out_shape=(
-                jax.ShapeDtypeStruct((rows, cols), bf16),
-                jax.ShapeDtypeStruct((rows, cols), bf16),
+                pltpu.VMEM((rows, cols), f32),
+                pltpu.VMEM((4, NUNIT, unit // 128, 128), f32),
                 jax.ShapeDtypeStruct((NCH, 2, rows // NCH, kb), bf16),
                 jax.ShapeDtypeStruct((rows, kb), bf16),
             ),
-            in_specs=[any_spec, any_spec, any_spec, pl.BlockSpec(memory_space=pltpu.VMEM)],
-            out_specs=(any_spec,) * 4,
+            in_specs=[any_spec, any_spec, any_spec],
+            out_specs=(vmem_spec, vmem_spec, any_spec, any_spec),
             scratch_shapes=[
                 pltpu.VMEM((2, kb, cols), bf16),
                 pltpu.VMEM((2, kb, cols), bf16),
-                pltpu.VMEM((rows, cols), f32),
                 pltpu.VMEM((2, 2, unit, kb), bf16),
                 pltpu.VMEM((2, unit, cols), bf16),
-                pltpu.VMEM((2, unit, cols), bf16),
                 pltpu.VMEM((NUNIT, unit // 128, 128), f32),
-                pltpu.VMEM((4, NUNIT, unit // 128, 128), f32),
                 dma((NCH,)), dma, dma, dma, dma,
                 dma((NWC,)), dma((NWC,)), dma, dma, dma,
                 dma, dma, dma, dma,
-                dma((2, 3)), dma, dma((2,)),
+                dma((2, 3)), dma,
                 dma((3,)), dma((4,)),
             ],
             compiler_params=pltpu.CompilerParams(
-                collective_id=0, has_side_effects=True, vmem_limit_bytes=64 * 1024 * 1024 - 65536),
-            name="gather_project_norm",
-        )(attn_blk, w_blk, res_blk, gain_blk.reshape(1, cols))
-        return outs[0], outs[1]
+                collective_id=0, has_side_effects=True, vmem_limit_bytes=44 * 1024 * 1024),
+            name="gather_project",
+        )(attn_blk, w_blk, res_blk)
+        return pl.pallas_call(
+            finish_kernel,
+            out_shape=(jax.ShapeDtypeStruct((rows, cols), bf16),) * 2,
+            in_specs=[vmem_spec, vmem_spec, vmem_spec],
+            out_specs=(any_spec, any_spec),
+            scratch_shapes=[pltpu.VMEM((2, unit, cols), bf16), pltpu.VMEM((2, unit, cols), bf16), dma((2, 2))],
+            compiler_params=pltpu.CompilerParams(vmem_limit_bytes=8 * 1024 * 1024),
+            name="norm_store",
+        )(h, ss, gain_blk.reshape(1, cols))
 
     row_spec = P(("dp", "tp"), "tp2")
     return jax.shard_map(local_step, mesh=mesh, in_specs=(P("dp", "tp"), P("tp", "tp2"), row_spec, P("tp2")), out_specs=(row_spec, row_spec), check_vma=False)

time: 301 us -> 284 us (0.944)
  local copies, waits for them, and re-layouts: 16.9 us -> 0.01 us
    unnamed x2, local copies, waits for them, and re-layouts: 16.9 us -> 0.01 us
    pallas_call x1 -> x2, Pallas kernels: 280 us -> 280 us  [the longest x1 273 us: local_step(): pl.pallas_call(kernel, out_shape=(pltpu.VMEM((rows, cols), f32), pltpu.VM...]
where the time goes in v2:
time: 284 us; the launch traced here: 281 us
  Pallas kernels  280 us (99%)
    pallas_call x1, Pallas kernels, local_step(): pl.pallas_call(kernel, out_shape=(pltpu.VMEM((rows, cols), f32), pltpu.VM...  273 us
    pallas_call x1, Pallas kernels, local_step(): pl.pallas_call(finish_kernel, out_shape=(jax.ShapeDtypeStruct((rows, cols...  7.41 us

profile of v2, /device:TPU:0, one launch (start us, length us, event | category | flops | bytes accessed | tf_op | source)
XLA Modules:
  0.0 280.8 jit_solution(11107082288102562585)
XLA Ops:
  0.6 0.0 copy-start
  0.6 272.7 %gather_project.1 = (f32[2048,2048]{1,0:T(8,128)S(1)}, f32[4,8,2,128]{3,2,1,0:T(2,128)S(1)}, bf16[32,2,64,2048]{3,2,1,0:T(8,128)(2,1)}, bf16[2048,2048]{1,0:T(8,128)(2,1)}) custom-call(bf16[8192,2048]{1,0:T(8,128)(2,1)} %a.1, bf16[2048,2048]{1,0:T(8,128)(2,1)} %w.1, bf16[2048,2048]{1,0:T(8,128)(2,1)} %r.1), custom_call_target="tpu_custom_call" | custom-call | tf_op jit(solution)/shard_map/gather_project/pallas_call | solution.py:377
  273.3 0.0 copy-done
  273.4 7.4 %norm_store.1 = (bf16[2048,2048]{1,0:T(8,128)(2,1)}, bf16[2048,2048]{1,0:T(8,128)(2,1)}) custom-call(f32[2048,2048]{1,0:T(8,128)S(1)} %get-tuple-element.4.h, f32[4,8,2,128]{3,2,1,0:T(2,128)S(1)} %get-tuple-element.5.ss, f32[1,2048]{1,0:T(1,128)S(1)} %bitcast.1), custom_call_target="tpu_custom_call" | custom-call | tf_op jit(solution)/shard_map/norm_store/pallas_call | solution.py:403
Async XLA Ops:
  0.6 272.7 %copy-start = (f32[2048]{0:T(1024)S(1)}, f32[2048]{0:T(1024)}, u32[]{:S(2)}) copy-start(f32[2048]{0:T(1024)} %param.7) | copy-start | bytes 24580

commit v3 on v2

--- a/solution.py
+++ b/solution.py
@@ -9,13 +9,19 @@
 
 EPS_NORM = 1e-6
 MESH = pl.DeviceIdType.MESH
-NCH = 32
+NCH = 64
+FAR = NCH // 4
+NEAR = NCH // 8
 NWC = 8
-GRP = 4
-NUNIT = NCH // GRP
-AHEAD = 3
-NSLOT = 21
-LOCAL0 = 2
+WS = 2 * NWC
+NUNIT = 8
+GRP = NCH // NUNIT
+AHEAD = 6
+NSLOT = 2 * FAR + NEAR + 1
+LOCAL0 = 6
+LOADS = 16
+WREADY = WS + 2
+COLS0 = FAR + 4
 
 
 def step_count(i, slots):
@@ -25,13 +31,13 @@
     return n
 
 
-END_UNITS = (10, 10, 12, 13, 16, 17, 19, 20)
-MID_UNITS = (17, 18, 19, 19, 19, 20, 20, 20)
+END_UNITS = (19, 20, 24, 25, 32, 33, 39, 40)
+MID_UNITS = (35, 36, 37, 38)
 
 
 def kernel(a, w, r, acc, ss_all, ax, ap, wl, wr, abuf, rbuf, ss_loc,
            recv_a, send_ya, send_yw, send_zi, send_zo, recv_wy, recv_wx, recv_wd, send_wx, send_wd,
-           recv_da, recv_dw, send_da, send_dw, load_sem, load_w, send_ss, recv_ss):
+           recv_da, recv_dw, send_da, send_dw, load_sem, load_w, load_a, send_ss, recv_ss):
     x = lax.axis_index("dp")
     z = lax.axis_index("tp2")
     t = lax.axis_index("tp")
@@ -40,7 +46,7 @@
     rows, cols = acc.shape
     kb = w.shape[0]
     ch = rows // NCH
-    wch = kb // 2 // NWC
+    wch = cols // NWC
     unit = ch * GRP
     side = z // 2
     end = (z == 0) | (z == 3)
@@ -70,7 +76,7 @@
     pl.semaphore_wait(barrier, 7)
 
     def mp(start, j):
-        return start + NCH // 4 + lax.rem(j + NCH // 8, NCH // 4)
+        return start + FAR + lax.rem(j + NEAR, FAR)
 
     def send_y_a(q):
         for cc in range(2):
@@ -78,28 +84,28 @@
             remote(a.at[pl.ds(pl.multiple_of(row, ch), ch)], ax.at[q, c], send_ya, recv_a.at[q],
                    (x, z, (1 - y) * 2 + cc)).start()
 
-    def w_rows(half, i):
-        return pl.ds(pl.multiple_of(half * (kb // 2) + i * wch, wch), wch)
-
-    def send_y_w(i):
-        remote(w.at[w_rows(x, i)], wr.at[c, w_rows(x, i)], send_yw, recv_wy.at[i], y_same).start()
+    def w_part(half, n):
+        return (pl.ds(pl.multiple_of(half * (kb // 2), kb // 2), kb // 2), pl.ds(pl.multiple_of(n * wch, wch), wch))
+
+    def send_y_w(n):
+        rs, cs = w_part(x, n)
+        remote(w.at[rs, cs], wr.at[c, rs, cs], send_yw, recv_wy.at[n], y_same).start()
 
     def y_sends(i):
-        @pl.when(end & (i < NWC))
-        def _():
-            send_y_w(i)
-
-        @pl.when(end & (i >= NWC) & (i < NWC + 12))
-        def _():
-            send_y_a(base + i - NWC)
-
-        @pl.when(mid & (i < 8))
-        def _():
-            send_y_a(mp(base, i))
-
-        @pl.when(mid & (i >= 8) & (i < 8 + NWC))
-        def _():
-            send_y_w(i - 8)
+        iw = jnp.where(end, i, i - FAR)
+        ia = jnp.where(end, i - WS, i)
+
+        @pl.when((iw >= 0) & (iw < WS) & (lax.rem(iw, 2) == 0))
+        def _():
+            send_y_w(iw // 2)
+
+        @pl.when(end & (ia >= 0) & (ia < FAR + NEAR))
+        def _():
+            send_y_a(base + ia)
+
+        @pl.when(mid & (ia < FAR))
+        def _():
+            send_y_a(mp(base, ia))
 
     lax.fori_loop(0, AHEAD, lambda i, _: (y_sends(i), None)[1], None)
 
@@ -109,8 +115,17 @@
     own_w = pltpu.make_async_copy(w, wl.at[0], load_w)
     own_w.start()
 
-    def arrive(q):
+    def load(q):
+        here = pl.ds(pl.multiple_of(q * ch, ch), ch)
+        for b in range(2):
+            pltpu.make_async_copy(ax.at[q, b], wl.at[b, here], load_a.at[q // GRP]).start()
+
+    def arrive(q, i):
         wait_bytes(ax.at[q], recv_a.at[q])
+
+        @pl.when(i >= LOADS)
+        def _():
+            load(q)
 
     def pass_in(q):
         remote(ax.at[q], ax.at[q], send_zi, recv_a.at[q], (x, z_in, t)).start()
@@ -118,91 +133,97 @@
     def pass_out(q):
         remote(ax.at[q], ax.at[q], send_zo, recv_a.at[q], (x, z_out, t)).start()
 
-    def w_from_y(i):
-        part = wr.at[c, w_rows(x, i)]
-        wait_bytes(part, recv_wy.at[i])
-        remote(part, part, send_wx, recv_wx.at[i], x_peer).start()
-        remote(part, part, send_wd, recv_wd, partner).start()
-
-    def w_from_x(i):
-        part = wr.at[c, w_rows(1 - x, i)]
-        wait_bytes(part, recv_wx.at[i])
-        remote(part, part, send_wd, recv_wd, partner).start()
+    def w_from_y(n):
+        rs, cs = w_part(x, n)
+        part = wr.at[c, rs, cs]
+        wait_bytes(part, recv_wy.at[n])
+        remote(part, part, send_wx, recv_wx.at[n], x_peer).start()
+        remote(part, part, send_wd, recv_wd.at[n], partner).start()
+
+    def w_from_x(n):
+        rs, cs = w_part(1 - x, n)
+        part = wr.at[c, rs, cs]
+        wait_bytes(part, recv_wx.at[n])
+        remote(part, part, send_wd, recv_wd.at[n], partner).start()
+
+    def w_from_partner(n):
+        cs = pl.ds(pl.multiple_of(n * wch, wch), wch)
+        wait_bytes(wr.at[1 - c, :, cs], recv_wd.at[n])
+
+    def z_chunk(j):
+        return jnp.where(j < NEAR, mp(base, j), jnp.where(j < NEAR + FAR, mp(other, j - NEAR), other + j - NEAR - FAR))
 
     def comm(i):
         y_sends(i + AHEAD)
+        iw = jnp.where(end, i, i - FAR)
+        odd = lax.rem(i, 2) == 1
+
+        @pl.when(odd & (iw >= 1) & (iw < WS))
+        def _():
+            w_from_y(iw // 2)
+
+        @pl.when(odd & (iw >= 3) & (iw < WS + 2))
+        def _():
+            w_from_x((iw - 3) // 2)
 
         @pl.when(end)
         def _():
-            @pl.when(i < NWC)
-            def _():
-                w_from_y(i)
-
-            @pl.when((i >= NWC) & (i < NWC + 12))
-            def _():
-                q = base + i - NWC
-                arrive(q)
-
-                @pl.when(i < NWC + 8)
+            @pl.when((i >= WS) & (i < WS + FAR + NEAR))
+            def _():
+                q = base + i - WS
+                arrive(q, i)
+
+                @pl.when(i < WS + FAR)
                 def _():
                     pass_in(q)
 
-            @pl.when((i >= 1) & (i < 1 + NWC))
-            def _():
-                w_from_x(i - 1)
-
-            j = i - 1
-
-            @pl.when((j >= 0) & (j < 4))
-            def _():
-                arrive(mp(base, j))
-
-            @pl.when((j >= 4) & (j < 12))
-            def _():
-                arrive(mp(other, j - 4))
-
-            @pl.when((j >= 12) & (j < 20))
-            def _():
-                arrive(other + j - 12)
+            @pl.when((i >= 1) & (i < 1 + 2 * FAR + NEAR))
+            def _():
+                arrive(z_chunk(i - 1), i)
 
         @pl.when(mid)
         def _():
-            @pl.when(i < 8)
+            @pl.when(i < FAR)
             def _():
                 q = mp(base, i)
-                arrive(q)
-
-                @pl.when(i < 4)
+                arrive(q, i)
+
+                @pl.when(i < NEAR)
                 def _():
                     pass_out(q)
 
                 pass_in(q)
 
-            @pl.when((i >= 1) & (i < 9))
+            @pl.when((i >= 1) & (i < 1 + FAR))
             def _():
                 q = mp(other, i - 1)
-                arrive(q)
+                arrive(q, i)
                 pass_out(q)
 
-            @pl.when((i >= 9) & (i < 17))
-            def _():
-                q = base + i - 9
-                arrive(q)
+            @pl.when((i >= WS + 1) & (i < WS + 1 + FAR))
+            def _():
+                q = base + i - WS - 1
+                arrive(q, i)
                 pass_in(q)
 
-            @pl.when((i >= 10) & (i < 18))
-            def _():
-                q = other + i - 10
-                arrive(q)
+            @pl.when((i >= WS + 2) & (i < WS + 2 + FAR))
+            def _():
+                q = other + i - WS - 2
+                arrive(q, i)
                 pass_out(q)
 
-            @pl.when((i >= 8) & (i < 8 + NWC))
-            def _():
-                w_from_y(i - 8)
-
-            @pl.when((i >= 9) & (i < 9 + NWC))
-            def _():
-                w_from_x(i - 9)
+    def early_loads():
+        def from_z(j, _):
+            load(jnp.where(end, z_chunk(j), mp(other, j)))
+            return None
+
+        lax.fori_loop(0, LOADS - 1, from_z, None)
+
+        def from_y(j, _):
+            load(mp(base, j))
+            return None
+
+        lax.fori_loop(0, jnp.where(end, 0, LOADS), from_y, None)
 
     tn = min(512, cols)
     ntile = cols // tn
@@ -236,46 +257,91 @@
 
         lax.fori_loop(0, ntile, tile, None)
 
+    gs = NUNIT // 2
+
     def unit_of(u):
-        gs = NUNIT // 2
         b = side * gs
         o = (1 - side) * gs
         end_order = (b + 3, o + 3, b, o + 2, b + 1, o, b + 2, o + 1)
-        mid_order = (b + 3, b + 2, o + 3, o + 2, b, o, b + 1, o + 1)
+        mid_order = (b, o, b + 1, o + 1, 0, 0, 0, 0)
         q = jnp.int32(0)
         for k in range(NUNIT):
             q = q + jnp.where(u == k, jnp.where(end, end_order[k], mid_order[k]), 0)
         return q
 
+    def wait_load(q):
+        here = pl.ds(pl.multiple_of(q * unit, unit), unit)
+        wait_bytes(wl.at[:, here], load_a.at[q])
+
+    def far_product(here, cs):
+        p0 = jnp.dot(wl[0, here, :], wr[0, :, cs], preferred_element_type=jnp.float32)
+        p1 = jnp.dot(wl[1, here, :], wr[1, :, cs], preferred_element_type=jnp.float32)
+        v = acc[here, cs] + (p0.astype(jnp.bfloat16).astype(jnp.float32) + p1.astype(jnp.bfloat16).astype(jnp.float32))
+        acc[here, cs] = v
+        return v
+
+    def squares(v):
+        sq = v * v
+        part = sq[:, :128]
+        for k in range(1, sq.shape[1] // 128):
+            part = part + sq[:, k * 128:(k + 1) * 128]
+        return part
+
+    def keep_squares(q, part):
+        for k in range(unit // 128):
+            ss_loc[q, k:k + 1, :] = jnp.sum(part[k * 128:(k + 1) * 128, :].T, axis=0, keepdims=True)
+
     def remote_unit(u, _):
         q = unit_of(u)
         here = pl.ds(pl.multiple_of(q * unit, unit), unit)
-        slot = lax.rem(u, 2)
-        loads = [pltpu.make_async_copy(ax.at[pl.ds(q * GRP, GRP), b], abuf.at[slot, b].reshape(GRP, ch, kb),
-                                       load_sem.at[slot, b]) for b in range(2)]
-        for cp in loads:
-            cp.start()
-
-        for cp in loads:
-            cp.wait()
+        wait_load(q)
 
         def tile(n, part):
             cs = pl.ds(pl.multiple_of(n * tn, tn), tn)
-            p0 = jnp.dot(abuf[slot, 0], wr[0, :, cs], preferred_element_type=jnp.float32)
-            p1 = jnp.dot(abuf[slot, 1], wr[1, :, cs], preferred_element_type=jnp.float32)
-            v = acc[here, cs] + (p0.astype(jnp.bfloat16).astype(jnp.float32) + p1.astype(jnp.bfloat16).astype(jnp.float32))
-            acc[here, cs] = v
-            sq = v * v
-            for k in range(tn // 128):
-                part = part + sq[:, k * 128:(k + 1) * 128]
-            return part
-
-        part = lax.fori_loop(0, ntile, tile, jnp.zeros((unit, 128), jnp.float32))
-        for k in range(unit // 128):
-            ss_loc[q, k:k + 1, :] = jnp.sum(part[k * 128:(k + 1) * 128, :].T, axis=0, keepdims=True)
+            return part + squares(far_product(here, cs))
+
+        keep_squares(q, lax.fori_loop(0, ntile, tile, jnp.zeros((unit, 128), jnp.float32)))
         return None
 
+    def column_unit(k):
+        return jnp.where(k < 2, side, 1 - side) * gs + 2 + lax.rem(k, 2)
+
+    def column_step(n):
+        w_from_partner(n)
+
+        @pl.when(n == 0)
+        def _():
+            for k in range(4):
+                wait_load(column_unit(jnp.int32(k)))
+
+        cs = pl.ds(pl.multiple_of(n * wch, wch), wch)
+
+        def rows_of(k, _):
+            here = pl.ds(pl.multiple_of(column_unit(k) * unit, unit), unit)
+            far_product(here, cs)
+            return None
+
+        lax.fori_loop(0, 4, rows_of, None)
+
+        @pl.when(n == NWC - 1)
+        def _():
+            def sums(k, _):
+                q = column_unit(k)
+                here = pl.ds(pl.multiple_of(q * unit, unit), unit)
+
+                def tile(m, part):
+                    return part + squares(acc[here, pl.ds(pl.multiple_of(m * tn, tn), tn)])
+
+                keep_squares(q, lax.fori_loop(0, ntile, tile, jnp.zeros((unit, 128), jnp.float32)))
+                return None
+
+            lax.fori_loop(0, 4, sums, None)
+
     def slot_body(i, _):
+        @pl.when(i == LOADS)
+        def _():
+            early_loads()
+
         comm(i)
 
         @pl.when(i == LOCAL0 - 1)
@@ -290,9 +356,15 @@
         def _():
             local_unit(i - LOCAL0)
 
-        @pl.when(i == jnp.where(end, END_UNITS[0], MID_UNITS[0]))
-        def _():
-            wait_bytes(wr.at[1 - c], recv_wd)
+        @pl.when(end & (i == WREADY))
+        def _():
+            lax.fori_loop(0, NWC, lambda n, _: (w_from_partner(n), None)[1], None)
+
+        jc = i - COLS0
+
+        @pl.when(mid & (jc >= 0) & (jc < WS) & (lax.rem(jc, 2) == 0))
+        def _():
+            column_step(jc // 2)
 
         lo = jnp.where(end, step_count(i - 1, END_UNITS), step_count(i - 1, MID_UNITS))
         hi = jnp.where(end, step_count(i, END_UNITS), step_count(i, MID_UNITS))
@@ -311,14 +383,14 @@
 
     @pl.when(end)
     def _():
-        wait_bytes(ax.at[pl.ds(0, 12)], send_ya)
-        wait_bytes(ax.at[pl.ds(0, 8)], send_zi)
+        wait_bytes(ax.at[pl.ds(0, FAR + NEAR)], send_ya)
+        wait_bytes(ax.at[pl.ds(0, FAR)], send_zi)
 
     @pl.when(mid)
     def _():
-        wait_bytes(ax.at[pl.ds(0, 8)], send_ya)
-        wait_bytes(ax.at[pl.ds(0, 16)], send_zi)
-        wait_bytes(ax.at[pl.ds(0, 20)], send_zo)
+        wait_bytes(ax.at[pl.ds(0, FAR)], send_ya)
+        wait_bytes(ax.at[pl.ds(0, 2 * FAR)], send_zi)
+        wait_bytes(ax.at[pl.ds(0, 2 * FAR + NEAR)], send_zo)
 
     for k in range(1, 4):
         src = lax.rem(z + k, 4)
@@ -391,9 +463,9 @@
                 pltpu.VMEM((2, unit, cols), bf16),
                 pltpu.VMEM((NUNIT, unit // 128, 128), f32),
                 dma((NCH,)), dma, dma, dma, dma,
-                dma((NWC,)), dma((NWC,)), dma, dma, dma,
+                dma((NWC,)), dma((NWC,)), dma((NWC,)), dma, dma,
                 dma, dma, dma, dma,
-                dma((2, 3)), dma,
+                dma((2, 3)), dma, dma((NUNIT,)),
                 dma((3,)), dma((4,)),
             ],
             compiler_params=pltpu.CompilerParams(

time: 284 us -> 275 us (0.968); the launches traced: 281 us -> 275 us
  Pallas kernels: 280 us -> 274 us
    pallas_call x1, Pallas kernels: 273 us -> 267 us  [local_step(): pl.pallas_call(kernel, out_shape=(pltpu.VMEM((rows, cols), f32), pltpu.VM...]
where the time goes in v3:
time: 275 us
  Pallas kernels  274 us (100%)
    pallas_call x1, Pallas kernels, local_step(): pl.pallas_call(kernel, out_shape=(pltpu.VMEM((rows, cols), f32), pltpu.VM...  267 us
    pallas_call x1, Pallas kernels, local_step(): pl.pallas_call(finish_kernel, out_shape=(jax.ShapeDtypeStruct((rows, cols...  7.41 us

profile of v3, /device:TPU:0, one launch (start us, length us, event | category | flops | bytes accessed | tf_op | source)
XLA Modules:
  0.0 274.8 jit_solution(5072091926000928722)
XLA Ops:
  0.6 0.0 copy-start
  0.6 266.8 %gather_project.1 = (f32[2048,2048]{1,0:T(8,128)S(1)}, f32[4,8,2,128]{3,2,1,0:T(2,128)S(1)}, bf16[64,2,32,2048]{3,2,1,0:T(8,128)(2,1)}, bf16[2048,2048]{1,0:T(8,128)(2,1)}) custom-call(bf16[8192,2048]{1,0:T(8,128)(2,1)} %a.1, bf16[2048,2048]{1,0:T(8,128)(2,1)} %w.1, bf16[2048,2048]{1,0:T(8,128)(2,1)} %r.1), custom_call_target="tpu_custom_call" | custom-call | tf_op jit(solution)/shard_map/gather_project/pallas_call | solution.py:449
  267.4 0.0 copy-done
  267.4 7.4 %norm_store.1 = (bf16[2048,2048]{1,0:T(8,128)(2,1)}, bf16[2048,2048]{1,0:T(8,128)(2,1)}) custom-call(f32[2048,2048]{1,0:T(8,128)S(1)} %get-tuple-element.4.h, f32[4,8,2,128]{3,2,1,0:T(2,128)S(1)} %get-tuple-element.5.ss, f32[1,2048]{1,0:T(1,128)S(1)} %bitcast.1), custom_call_target="tpu_custom_call" | custom-call | tf_op jit(solution)/shard_map/norm_store/pallas_call | solution.py:475
Async XLA Ops:
  0.6 266.8 %copy-start = (f32[2048]{0:T(1024)S(1)}, f32[2048]{0:T(1024)}, u32[]{:S(2)}) copy-start(f32[2048]{0:T(1024)} %param.7) | copy-start | bytes 24580

commit v4 on v3

--- a/solution.py
+++ b/solution.py
@@ -16,7 +16,7 @@
 WS = 2 * NWC
 NUNIT = 8
 GRP = NCH // NUNIT
-AHEAD = 6
+AHEAD = 12
 NSLOT = 2 * FAR + NEAR + 1
 LOCAL0 = 6
 LOADS = 16
@@ -151,7 +151,9 @@
         wait_bytes(wr.at[1 - c, :, cs], recv_wd.at[n])
 
     def z_chunk(j):
-        return jnp.where(j < NEAR, mp(base, j), jnp.where(j < NEAR + FAR, mp(other, j - NEAR), other + j - NEAR - FAR))
+        own = (j == 0) | (lax.rem(j, 2) == 1)
+        first = jnp.where(own, mp(base, (j + 1) // 2), mp(other, j // 2 - 1))
+        return jnp.where(j < 2 * NEAR - 1, first, jnp.where(j < NEAR + FAR, mp(other, j - NEAR), other + j - NEAR - FAR))
 
     def comm(i):
         y_sends(i + AHEAD)

time: 275 us -> 258 us (0.938)
  Pallas kernels: 274 us -> 255 us
    pallas_call x1, Pallas kernels: 267 us -> 247 us  [local_step(): pl.pallas_call(kernel, out_shape=(pltpu.VMEM((rows, cols), f32), pltpu.VM...]
where the time goes in v4:
time: 258 us; the launch traced here: 255 us
  Pallas kernels  255 us (99%)
    pallas_call x1, Pallas kernels, local_step(): pl.pallas_call(kernel, out_shape=(pltpu.VMEM((rows, cols), f32), pltpu.VM...  247 us
    pallas_call x1, Pallas kernels, local_step(): pl.pallas_call(finish_kernel, out_shape=(jax.ShapeDtypeStruct((rows, cols...  7.41 us

profile of v4, /device:TPU:0, one launch (start us, length us, event | category | flops | bytes accessed | tf_op | source)
XLA Modules:
  0.0 255.2 jit_solution(9264532167615042289)
XLA Ops:
  0.6 0.0 copy-start
  0.6 247.2 %gather_project.1 = (f32[2048,2048]{1,0:T(8,128)S(1)}, f32[4,8,2,128]{3,2,1,0:T(2,128)S(1)}, bf16[64,2,32,2048]{3,2,1,0:T(8,128)(2,1)}, bf16[2048,2048]{1,0:T(8,128)(2,1)}) custom-call(bf16[8192,2048]{1,0:T(8,128)(2,1)} %a.1, bf16[2048,2048]{1,0:T(8,128)(2,1)} %w.1, bf16[2048,2048]{1,0:T(8,128)(2,1)} %r.1), custom_call_target="tpu_custom_call" | custom-call | tf_op jit(solution)/shard_map/gather_project/pallas_call | solution.py:451
  247.8 0.0 copy-done
  247.8 7.4 %norm_store.1 = (bf16[2048,2048]{1,0:T(8,128)(2,1)}, bf16[2048,2048]{1,0:T(8,128)(2,1)}) custom-call(f32[2048,2048]{1,0:T(8,128)S(1)} %get-tuple-element.4.h, f32[4,8,2,128]{3,2,1,0:T(2,128)S(1)} %get-tuple-element.5.ss, f32[1,2048]{1,0:T(1,128)S(1)} %bitcast.1), custom_call_target="tpu_custom_call" | custom-call | tf_op jit(solution)/shard_map/norm_store/pallas_call | solution.py:477
Async XLA Ops:
  0.6 247.2 %copy-start = (f32[2048]{0:T(1024)S(1)}, f32[2048]{0:T(1024)}, u32[]{:S(2)}) copy-start(f32[2048]{0:T(1024)} %param.7) | copy-start | bytes 24580

commit v5 on v4

--- a/solution.py
+++ b/solution.py
@@ -15,7 +15,11 @@
 NWC = 8
 WS = 2 * NWC
 NUNIT = 8
+NHALF = 2 * NUNIT
 GRP = NCH // NUNIT
+HGRP = NCH // NHALF
+NBUF = 4
+NSUB = 4
 AHEAD = 12
 NSLOT = 2 * FAR + NEAR + 1
 LOCAL0 = 6
@@ -31,13 +35,13 @@
     return n
 
 
-END_UNITS = (19, 20, 24, 25, 32, 33, 39, 40)
-MID_UNITS = (35, 36, 37, 38)
+END_UNITS = (19, 19, 20, 20, 21, 22, 24, 25, 28, 29, 32, 33, 36, 37, 39, 40)
+MID_UNITS = (35, 35, 36, 36, 37, 37, 38, 38)
 
 
 def kernel(a, w, r, acc, ss_all, ax, ap, wl, wr, abuf, rbuf, ss_loc,
            recv_a, send_ya, send_yw, send_zi, send_zo, recv_wy, recv_wx, recv_wd, send_wx, send_wd,
-           recv_da, recv_dw, send_da, send_dw, load_sem, load_w, load_a, send_ss, recv_ss):
+           recv_da, recv_dw, send_da, send_dw, load_sem, load_w, load_a, recv_sub, send_ss, recv_ss):
     x = lax.axis_index("dp")
     z = lax.axis_index("tp2")
     t = lax.axis_index("tp")
@@ -48,6 +52,8 @@
     ch = rows // NCH
     wch = cols // NWC
     unit = ch * GRP
+    half = ch * HGRP
+    sub = ch // NSUB
     side = z // 2
     end = (z == 0) | (z == 3)
     mid = (z == 1) | (z == 2)
@@ -84,8 +90,15 @@
             remote(a.at[pl.ds(pl.multiple_of(row, ch), ch)], ax.at[q, c], send_ya, recv_a.at[q],
                    (x, z, (1 - y) * 2 + cc)).start()
 
-    def w_part(half, n):
-        return (pl.ds(pl.multiple_of(half * (kb // 2), kb // 2), kb // 2), pl.ds(pl.multiple_of(n * wch, wch), wch))
+    def send_y_first(q):
+        for k in range(NSUB):
+            for cc in range(2):
+                row = ((1 - y) * 2 + cc) * rows + q * ch + k * sub
+                remote(a.at[pl.ds(pl.multiple_of(row, sub), sub)], ax.at[q, c, pl.ds(k * sub, sub)], send_ya,
+                       recv_sub.at[k], (x, z, (1 - y) * 2 + cc)).start()
+
+    def w_part(part, n):
+        return (pl.ds(pl.multiple_of(part * (kb // 2), kb // 2), kb // 2), pl.ds(pl.multiple_of(n * wch, wch), wch))
 
     def send_y_w(n):
         rs, cs = w_part(x, n)
@@ -103,7 +116,11 @@
         def _():
             send_y_a(base + ia)
 
-        @pl.when(mid & (ia < FAR))
+        @pl.when(mid & (ia == 0))
+        def _():
+            send_y_first(mp(base, 0))
+
+        @pl.when(mid & (ia >= 1) & (ia < FAR))
         def _():
             send_y_a(mp(base, ia))
 
@@ -118,7 +135,7 @@
     def load(q):
         here = pl.ds(pl.multiple_of(q * ch, ch), ch)
         for b in range(2):
-            pltpu.make_async_copy(ax.at[q, b], wl.at[b, here], load_a.at[q // GRP]).start()
+            pltpu.make_async_copy(ax.at[q, b], wl.at[b, here], load_a.at[q // HGRP]).start()
 
     def arrive(q, i):
         wait_bytes(ax.at[q], recv_a.at[q])
@@ -185,7 +202,16 @@
 
         @pl.when(mid)
         def _():
-            @pl.when(i < FAR)
+            @pl.when(i == 0)
+            def _():
+                q = mp(base, 0)
+                for k in range(NSUB):
+                    piece = ax.at[q, :, pl.ds(k * sub, sub)]
+                    wait_bytes(piece, recv_sub.at[k])
+                    remote(piece, piece, send_zo, recv_a.at[q], (x, z_out, t)).start()
+                pass_in(q)
+
+            @pl.when((i >= 1) & (i < FAR))
             def _():
                 q = mp(base, i)
                 arrive(q, i)
@@ -262,17 +288,17 @@
     gs = NUNIT // 2
 
     def unit_of(u):
-        b = side * gs
-        o = (1 - side) * gs
-        end_order = (b + 3, o + 3, b, o + 2, b + 1, o, b + 2, o + 1)
-        mid_order = (b, o, b + 1, o + 1, 0, 0, 0, 0)
+        b = side * NUNIT
+        o = (1 - side) * NUNIT
+        end_order = (b + 6, b + 7, o + 6, o + 7, b, o + 4, b + 1, o + 5, b + 2, o, b + 3, o + 1, b + 4, o + 2, b + 5, o + 3)
+        mid_order = (b, b + 1, o, o + 1, b + 2, b + 3, o + 2, o + 3) + (0,) * NUNIT
         q = jnp.int32(0)
-        for k in range(NUNIT):
+        for k in range(NHALF):
             q = q + jnp.where(u == k, jnp.where(end, end_order[k], mid_order[k]), 0)
         return q
 
     def wait_load(q):
-        here = pl.ds(pl.multiple_of(q * unit, unit), unit)
+        here = pl.ds(pl.multiple_of(q * half, half), half)
         wait_bytes(wl.at[:, here], load_a.at[q])
 
     def far_product(here, cs):
@@ -290,19 +316,18 @@
         return part
 
     def keep_squares(q, part):
-        for k in range(unit // 128):
-            ss_loc[q, k:k + 1, :] = jnp.sum(part[k * 128:(k + 1) * 128, :].T, axis=0, keepdims=True)
+        ss_loc[q] = jnp.sum(part.T, axis=0, keepdims=True)
 
     def remote_unit(u, _):
         q = unit_of(u)
-        here = pl.ds(pl.multiple_of(q * unit, unit), unit)
+        here = pl.ds(pl.multiple_of(q * half, half), half)
         wait_load(q)
 
         def tile(n, part):
             cs = pl.ds(pl.multiple_of(n * tn, tn), tn)
             return part + squares(far_product(here, cs))
 
-        keep_squares(q, lax.fori_loop(0, ntile, tile, jnp.zeros((unit, 128), jnp.float32)))
+        keep_squares(q, lax.fori_loop(0, ntile, tile, jnp.zeros((half, 128), jnp.float32)))
         return None
 
     def column_unit(k):
@@ -314,7 +339,8 @@
         @pl.when(n == 0)
         def _():
             for k in range(4):
-                wait_load(column_unit(jnp.int32(k)))
+                for e in range(2):
+                    wait_load(column_unit(jnp.int32(k)) * 2 + e)
 
         cs = pl.ds(pl.multiple_of(n * wch, wch), wch)
 
@@ -328,16 +354,16 @@
         @pl.when(n == NWC - 1)
         def _():
             def sums(k, _):
-                q = column_unit(k)
-                here = pl.ds(pl.multiple_of(q * unit, unit), unit)
+                q = column_unit(k // 2) * 2 + lax.rem(k, 2)
+                here = pl.ds(pl.multiple_of(q * half, half), half)
 
                 def tile(m, part):
                     return part + squares(acc[here, pl.ds(pl.multiple_of(m * tn, tn), tn)])
 
-                keep_squares(q, lax.fori_loop(0, ntile, tile, jnp.zeros((unit, 128), jnp.float32)))
+                keep_squares(q, lax.fori_loop(0, ntile, tile, jnp.zeros((half, 128), jnp.float32)))
                 return None
 
-            lax.fori_loop(0, 4, sums, None)
+            lax.fori_loop(0, 8, sums, None)
 
     def slot_body(i, _):
         @pl.when(i == LOADS)
@@ -402,41 +428,43 @@
 
 def finish_kernel(h, ss, g, h_out, n_out, hbuf, nbuf, sem):
     rows, cols = h.shape
-    unit = rows // NUNIT
-    nfin = NUNIT
+    step_rows = rows // NHALF
 
     def copies(q):
-        slot = lax.rem(q, 2)
-        here = pl.ds(pl.multiple_of(q * unit, unit), unit)
+        slot = lax.rem(q, NBUF)
+        here = pl.ds(pl.multiple_of(q * step_rows, step_rows), step_rows)
         return (pltpu.make_async_copy(hbuf.at[slot], h_out.at[here], sem.at[slot, 0]),
                 pltpu.make_async_copy(nbuf.at[slot], n_out.at[here], sem.at[slot, 1]))
 
     def step(q, _):
-        slot = lax.rem(q, 2)
-
-        @pl.when(q >= 2)
-        def _():
-            for cp in copies(q - 2):
+        slot = lax.rem(q, NBUF)
+
+        @pl.when(q >= NBUF)
+        def _():
+            for cp in copies(q - NBUF):
                 cp.wait()
 
         total = ss[0, q] + ss[1, q] + ss[2, q] + ss[3, q]
         inv = lax.rsqrt(total / (cols * 4) + EPS_NORM)
-        for k in range(unit // 128):
-            col = jnp.broadcast_to(inv[k:k + 1, :], (128, 128)).T
-            rs = pl.ds(pl.multiple_of(q * unit + k * 128, 128), 128)
-            for m in range(cols // 128):
-                cs = slice(m * 128, (m + 1) * 128)
-                v = h[rs, cs]
-                hbuf[slot, k * 128:(k + 1) * 128, cs] = v.astype(jnp.bfloat16)
-                nbuf[slot, k * 128:(k + 1) * 128, cs] = (v * col * g[:, cs]).astype(jnp.bfloat16)
+        col = jnp.broadcast_to(inv, (128, 128)).T
+        rs = pl.ds(pl.multiple_of(q * 128, 128), 128)
+        for m in range(cols // 128):
+            cs = slice(m * 128, (m + 1) * 128)
+            v = h[rs, cs]
+            hbuf[slot, :, cs] = v.astype(jnp.bfloat16)
+            nbuf[slot, :, cs] = (v * col * g[:, cs]).astype(jnp.bfloat16)
         for cp in copies(q):
             cp.start()
         return None
 
-    lax.fori_loop(0, nfin, step, None)
-    for q in (nfin - 2, nfin - 1):
-        for cp in copies(jnp.int32(q)):
+    lax.fori_loop(0, NHALF, step, None)
+
+    def drain(q, _):
+        for cp in copies(q):
             cp.wait()
+        return None
+
+    lax.fori_loop(NHALF - NBUF, NHALF, drain, None)
 
 
 def solution(mesh):
@@ -452,7 +480,7 @@
             kernel,
             out_shape=(
                 pltpu.VMEM((rows, cols), f32),
-                pltpu.VMEM((4, NUNIT, unit // 128, 128), f32),
+                pltpu.VMEM((4, NHALF, 1, 128), f32),
                 jax.ShapeDtypeStruct((NCH, 2, rows // NCH, kb), bf16),
                 jax.ShapeDtypeStruct((rows, kb), bf16),
             ),
@@ -463,11 +491,11 @@
                 pltpu.VMEM((2, kb, cols), bf16),
                 pltpu.VMEM((2, 2, unit, kb), bf16),
                 pltpu.VMEM((2, unit, cols), bf16),
-                pltpu.VMEM((NUNIT, unit // 128, 128), f32),
+                pltpu.VMEM((NHALF, 1, 128), f32),
                 dma((NCH,)), dma, dma, dma, dma,
                 dma((NWC,)), dma((NWC,)), dma((NWC,)), dma, dma,
                 dma, dma, dma, dma,
-                dma((2, 3)), dma, dma((NUNIT,)),
+                dma((2, 3)), dma, dma((NHALF,)), dma((NSUB,)),
                 dma((3,)), dma((4,)),
             ],
             compiler_params=pltpu.CompilerParams(
@@ -479,7 +507,7 @@
             out_shape=(jax.ShapeDtypeStruct((rows, cols), bf16),) * 2,
             in_specs=[vmem_spec, vmem_spec, vmem_spec],
             out_specs=(any_spec, any_spec),
-            scratch_shapes=[pltpu.VMEM((2, unit, cols), bf16), pltpu.VMEM((2, unit, cols), bf16), dma((2, 2))],
+            scratch_shapes=[pltpu.VMEM((NBUF, rows // NHALF, cols), bf16)] * 2 + [dma((NBUF, 2))],
             compiler_params=pltpu.CompilerParams(vmem_limit_bytes=8 * 1024 * 1024),
             name="norm_store",
         )(h, ss, gain_blk.reshape(1, cols))

time: 258 us -> 252 us (0.977); the launches traced: 255 us -> 252 us
  Pallas kernels: 255 us -> 252 us
where the time goes in v5:
time: 252 us
  Pallas kernels  252 us (100%)
    pallas_call x1, Pallas kernels, local_step(): pl.pallas_call(kernel, out_shape=(pltpu.VMEM((rows, cols), f32), pltpu.VM...  246 us
    pallas_call x1, Pallas kernels, local_step(): pl.pallas_call(finish_kernel, out_shape=(jax.ShapeDtypeStruct((rows, cols...  6.08 us

profile of v5, /device:TPU:0, one launch (start us, length us, event | category | flops | bytes accessed | tf_op | source)
XLA Modules:
  0.0 252.3 jit_solution(776642623116709995)
XLA Ops:
  0.6 0.0 copy-start
  0.6 245.6 %gather_project.1 = (f32[2048,2048]{1,0:T(8,128)S(1)}, f32[4,16,1,128]{3,2,1,0:T(1,128)S(1)}, bf16[64,2,32,2048]{3,2,1,0:T(8,128)(2,1)}, bf16[2048,2048]{1,0:T(8,128)(2,1)}) custom-call(bf16[8192,2048]{1,0:T(8,128)(2,1)} %a.1, bf16[2048,2048]{1,0:T(8,128)(2,1)} %w.1, bf16[2048,2048]{1,0:T(8,128)(2,1)} %r.1), custom_call_target="tpu_custom_call" | custom-call | tf_op jit(solution)/shard_map/gather_project/pallas_call | solution.py:479
  246.2 0.0 copy-done
  246.2 6.1 %norm_store.1 = (bf16[2048,2048]{1,0:T(8,128)(2,1)}, bf16[2048,2048]{1,0:T(8,128)(2,1)}) custom-call(f32[2048,2048]{1,0:T(8,128)S(1)} %get-tuple-element.4.h, f32[4,16,1,128]{3,2,1,0:T(1,128)S(1)} %get-tuple-element.5.ss, f32[1,2048]{1,0:T(1,128)S(1)} %bitcast.1), custom_call_target="tpu_custom_call" | custom-call | tf_op jit(solution)/shard_map/norm_store/pallas_call | solution.py:505
Async XLA Ops:
  0.6 245.6 %copy-start = (f32[2048]{0:T(1024)S(1)}, f32[2048]{0:T(1024)}, u32[]{:S(2)}) copy-start(f32[2048]{0:T(1024)} %param.7) | copy-start | bytes 24580

commit v6 on v5

--- a/solution.py
+++ b/solution.py
@@ -18,7 +18,9 @@
 NHALF = 2 * NUNIT
 GRP = NCH // NUNIT
 HGRP = NCH // NHALF
+LATE = FAR // 2
 NBUF = 4
+NDIRECT = 2
 NSUB = 4
 AHEAD = 12
 NSLOT = 2 * FAR + NEAR + 1
@@ -41,7 +43,7 @@
 
 def kernel(a, w, r, acc, ss_all, ax, ap, wl, wr, abuf, rbuf, ss_loc,
            recv_a, send_ya, send_yw, send_zi, send_zo, recv_wy, recv_wx, recv_wd, send_wx, send_wd,
-           recv_da, recv_dw, send_da, send_dw, load_sem, load_w, load_a, recv_sub, send_ss, recv_ss):
+           recv_da, recv_dw, send_da, send_dw, load_sem, load_w, load_a, recv_sub, send_first, credit_z, credit_y, send_ss, recv_ss):
     x = lax.axis_index("dp")
     z = lax.axis_index("tp2")
     t = lax.axis_index("tp")
@@ -79,18 +81,30 @@
         pl.semaphore_signal(barrier, inc=1, device_id=dev, device_id_type=MESH)
     for k in range(1, 4):
         pl.semaphore_signal(barrier, inc=1, device_id=(x, lax.rem(z + k, 4), t), device_id_type=MESH)
-    pl.semaphore_wait(barrier, 7)
+    z_mate = jnp.where(end, z_in, z_out)
+    for cc in range(2):
+        pl.semaphore_signal(barrier, inc=1, device_id=(x, z_mate, (1 - y) * 2 + cc), device_id_type=MESH)
+    pl.semaphore_wait(barrier, 9)
 
     def mp(start, j):
         return start + FAR + lax.rem(j + NEAR, FAR)
 
-    def send_y_a(q):
+    def chunk_rows(q):
+        return pl.ds(pl.multiple_of(q * ch, ch), ch)
+
+    def send_y_a(q, dst=None):
+        dst = ax.at[q, c] if dst is None else dst
         for cc in range(2):
             row = ((1 - y) * 2 + cc) * rows + q * ch
-            remote(a.at[pl.ds(pl.multiple_of(row, ch), ch)], ax.at[q, c], send_ya, recv_a.at[q],
+            remote(a.at[pl.ds(pl.multiple_of(row, ch), ch)], dst, send_ya, recv_a.at[q],
                    (x, z, (1 - y) * 2 + cc)).start()
 
     def send_y_first(q):
+        for k in range(NDIRECT):
+            for cc in range(2):
+                row = ((1 - y) * 2 + cc) * rows + q * ch + k * sub
+                remote(a.at[pl.ds(pl.multiple_of(row, sub), sub)], ax.at[q, c, pl.ds(k * sub, sub)], send_first,
+                       recv_a.at[q], (x, z_out, (1 - y) * 2 + cc)).start()
         for k in range(NSUB):
             for cc in range(2):
                 row = ((1 - y) * 2 + cc) * rows + q * ch + k * sub
@@ -112,9 +126,17 @@
         def _():
             send_y_w(iw // 2)
 
-        @pl.when(end & (ia >= 0) & (ia < FAR + NEAR))
+        @pl.when(end & (ia >= 0) & (ia < FAR))
         def _():
             send_y_a(base + ia)
+
+        @pl.when(end & (ia == FAR))
+        def _():
+            pl.semaphore_wait(credit_y, 2)
+
+        @pl.when(end & (ia >= FAR) & (ia < FAR + NEAR))
+        def _():
+            send_y_a(base + ia, wl.at[c, chunk_rows(base + ia)])
 
         @pl.when(mid & (ia == 0))
         def _():
@@ -143,6 +165,12 @@
         @pl.when(i >= LOADS)
         def _():
             load(q)
+
+    def arrive_late(q):
+        wait_bytes(wl.at[:, chunk_rows(q)], recv_a.at[q])
+
+    def pass_out_late(q):
+        remote(ax.at[q], wl.at[:, chunk_rows(q)], send_zo, recv_a.at[q], (x, z_out, t)).start()
 
     def pass_in(q):
         remote(ax.at[q], ax.at[q], send_zi, recv_a.at[q], (x, z_in, t)).start()
@@ -187,18 +215,25 @@
 
         @pl.when(end)
         def _():
-            @pl.when((i >= WS) & (i < WS + FAR + NEAR))
+            @pl.when((i >= WS) & (i < WS + FAR))
             def _():
                 q = base + i - WS
                 arrive(q, i)
-
-                @pl.when(i < WS + FAR)
-                def _():
-                    pass_in(q)
-
-            @pl.when((i >= 1) & (i < 1 + 2 * FAR + NEAR))
+                pass_in(q)
+
+            @pl.when((i >= WS + FAR) & (i < WS + FAR + NEAR))
+            def _():
+                arrive_late(base + i - WS)
+
+            nlate = 1 + 2 * FAR + NEAR - LATE
+
+            @pl.when((i >= 1) & (i < nlate))
             def _():
                 arrive(z_chunk(i - 1), i)
+
+            @pl.when((i >= nlate) & (i < nlate + LATE))
+            def _():
+                arrive_late(z_chunk(i - 1))
 
         @pl.when(mid)
         def _():
@@ -208,7 +243,8 @@
                 for k in range(NSUB):
                     piece = ax.at[q, :, pl.ds(k * sub, sub)]
                     wait_bytes(piece, recv_sub.at[k])
-                    remote(piece, piece, send_zo, recv_a.at[q], (x, z_out, t)).start()
+                    if k >= NDIRECT:
+                        remote(piece, piece, send_first, recv_a.at[q], (x, z_out, t)).start()
                 pass_in(q)
 
             @pl.when((i >= 1) & (i < FAR))
@@ -238,7 +274,18 @@
             def _():
                 q = other + i - WS - 2
                 arrive(q, i)
-                pass_out(q)
+
+                @pl.when(i < WS + 2 + FAR - LATE)
+                def _():
+                    pass_out(q)
+
+                @pl.when(i == WS + 2 + FAR - LATE)
+                def _():
+                    pl.semaphore_wait(credit_z, 1)
+
+                @pl.when(i >= WS + 2 + FAR - LATE)
+                def _():
+                    pass_out_late(q)
 
     def early_loads():
         def from_z(j, _):
@@ -321,7 +368,10 @@
     def remote_unit(u, _):
         q = unit_of(u)
         here = pl.ds(pl.multiple_of(q * half, half), half)
-        wait_load(q)
+
+        @pl.when(mid | (u < NHALF - 4))
+        def _():
+            wait_load(q)
 
         def tile(n, part):
             cs = pl.ds(pl.multiple_of(n * tn, tn), tn)
@@ -369,6 +419,12 @@
         @pl.when(i == LOADS)
         def _():
             early_loads()
+
+        @pl.when(end & (i == LOADS))
+        def _():
+            pl.semaphore_signal(credit_z, inc=1, device_id=(x, z_in, t), device_id_type=MESH)
+            for cc in range(2):
+                pl.semaphore_signal(credit_y, inc=1, device_id=(x, z, (1 - y) * 2 + cc), device_id_type=MESH)
 
         comm(i)
 
@@ -418,7 +474,8 @@
     def _():
         wait_bytes(ax.at[pl.ds(0, FAR)], send_ya)
         wait_bytes(ax.at[pl.ds(0, 2 * FAR)], send_zi)
-        wait_bytes(ax.at[pl.ds(0, 2 * FAR + NEAR)], send_zo)
+        wait_bytes(ax.at[pl.ds(0, 2 * FAR + NEAR - 1)], send_zo)
+        wait_bytes(ax.at[0], send_first)
 
     for k in range(1, 4):
         src = lax.rem(z + k, 4)
@@ -495,7 +552,8 @@
                 dma((NCH,)), dma, dma, dma, dma,
                 dma((NWC,)), dma((NWC,)), dma((NWC,)), dma, dma,
                 dma, dma, dma, dma,
-                dma((2, 3)), dma, dma((NHALF,)), dma((NSUB,)),
+                dma((2, 3)), dma, dma((NHALF,)), dma((NSUB,)), dma,
+                pltpu.SemaphoreType.REGULAR, pltpu.SemaphoreType.REGULAR,
                 dma((3,)), dma((4,)),
             ],
             compiler_params=pltpu.CompilerParams(

time: 252 us -> 252 us (level)
  no operation moved by 1% of the time
where the time goes in v6:
time: 252 us
  Pallas kernels  251 us (100%)
    pallas_call x1, Pallas kernels, local_step(): pl.pallas_call(kernel, out_shape=(pltpu.VMEM((rows, cols), f32), pltpu.VM...  245 us
    pallas_call x1, Pallas kernels, local_step(): pl.pallas_call(finish_kernel, out_shape=(jax.ShapeDtypeStruct((rows, cols...  6.08 us

profile of v6, /device:TPU:0, one launch (start us, length us, event | category | flops | bytes accessed | tf_op | source)
XLA Modules:
  0.0 251.9 jit_solution(1021730390681534396)
XLA Ops:
  0.6 0.0 copy-start
  0.6 245.1 %gather_project.1 = (f32[2048,2048]{1,0:T(8,128)S(1)}, f32[4,16,1,128]{3,2,1,0:T(1,128)S(1)}, bf16[64,2,32,2048]{3,2,1,0:T(8,128)(2,1)}, bf16[2048,2048]{1,0:T(8,128)(2,1)}) custom-call(bf16[8192,2048]{1,0:T(8,128)(2,1)} %a.1, bf16[2048,2048]{1,0:T(8,128)(2,1)} %w.1, bf16[2048,2048]{1,0:T(8,128)(2,1)} %r.1), custom_call_target="tpu_custom_call" | custom-call | tf_op jit(solution)/shard_map/gather_project/pallas_call | solution.py:536
  245.8 0.0 copy-done
  245.8 6.1 %norm_store.1 = (bf16[2048,2048]{1,0:T(8,128)(2,1)}, bf16[2048,2048]{1,0:T(8,128)(2,1)}) custom-call(f32[2048,2048]{1,0:T(8,128)S(1)} %get-tuple-element.4.h, f32[4,16,1,128]{3,2,1,0:T(1,128)S(1)} %get-tuple-element.5.ss, f32[1,2048]{1,0:T(1,128)S(1)} %bitcast.1), custom_call_target="tpu_custom_call" | custom-call | tf_op jit(solution)/shard_map/norm_store/pallas_call | solution.py:563
Async XLA Ops:
  0.6 245.1 %copy-start = (f32[2048]{0:T(1024)S(1)}, f32[2048]{0:T(1024)}, u32[]{:S(2)}) copy-start(f32[2048]{0:T(1024)} %param.7) | copy-start | bytes 24580

commit v7 on v6

--- a/solution.py
+++ b/solution.py
@@ -21,6 +21,7 @@
 LATE = FAR // 2
 NBUF = 4
 NDIRECT = 2
+PIECES = (2, 3, 0, 1)
 NSUB = 4
 AHEAD = 12
 NSLOT = 2 * FAR + NEAR + 1
@@ -43,7 +44,7 @@
 
 def kernel(a, w, r, acc, ss_all, ax, ap, wl, wr, abuf, rbuf, ss_loc,
            recv_a, send_ya, send_yw, send_zi, send_zo, recv_wy, recv_wx, recv_wd, send_wx, send_wd,
-           recv_da, recv_dw, send_da, send_dw, load_sem, load_w, load_a, recv_sub, send_first, credit_z, credit_y, send_ss, recv_ss):
+           recv_da, recv_dw, send_da, send_dw, load_sem, load_w, load_a, recv_sub, send_first, send_pieces, credit_z, credit_y, send_ss, recv_ss):
     x = lax.axis_index("dp")
     z = lax.axis_index("tp2")
     t = lax.axis_index("tp")
@@ -81,10 +82,7 @@
         pl.semaphore_signal(barrier, inc=1, device_id=dev, device_id_type=MESH)
     for k in range(1, 4):
         pl.semaphore_signal(barrier, inc=1, device_id=(x, lax.rem(z + k, 4), t), device_id_type=MESH)
-    z_mate = jnp.where(end, z_in, z_out)
-    for cc in range(2):
-        pl.semaphore_signal(barrier, inc=1, device_id=(x, z_mate, (1 - y) * 2 + cc), device_id_type=MESH)
-    pl.semaphore_wait(barrier, 9)
+    pl.semaphore_wait(barrier, 7)
 
     def mp(start, j):
         return start + FAR + lax.rem(j + NEAR, FAR)
@@ -99,17 +97,12 @@
             remote(a.at[pl.ds(pl.multiple_of(row, ch), ch)], dst, send_ya, recv_a.at[q],
                    (x, z, (1 - y) * 2 + cc)).start()
 
-    def send_y_first(q):
-        for k in range(NDIRECT):
+    def send_y_pieces(q, pieces, recv):
+        for k in pieces:
             for cc in range(2):
                 row = ((1 - y) * 2 + cc) * rows + q * ch + k * sub
                 remote(a.at[pl.ds(pl.multiple_of(row, sub), sub)], ax.at[q, c, pl.ds(k * sub, sub)], send_first,
-                       recv_a.at[q], (x, z_out, (1 - y) * 2 + cc)).start()
-        for k in range(NSUB):
-            for cc in range(2):
-                row = ((1 - y) * 2 + cc) * rows + q * ch + k * sub
-                remote(a.at[pl.ds(pl.multiple_of(row, sub), sub)], ax.at[q, c, pl.ds(k * sub, sub)], send_ya,
-                       recv_sub.at[k], (x, z, (1 - y) * 2 + cc)).start()
+                       recv(k), (x, z, (1 - y) * 2 + cc)).start()
 
     def w_part(part, n):
         return (pl.ds(pl.multiple_of(part * (kb // 2), kb // 2), kb // 2), pl.ds(pl.multiple_of(n * wch, wch), wch))
@@ -140,7 +133,13 @@
 
         @pl.when(mid & (ia == 0))
         def _():
-            send_y_first(mp(base, 0))
+            q = mp(base, 0)
+            send_y_pieces(q, PIECES, lambda k: recv_sub.at[k])
+
+        @pl.when(end & (i == 0))
+        def _():
+            q = mp(base, 0)
+            send_y_pieces(q, range(NDIRECT), lambda k: recv_a.at[q])
 
         @pl.when(mid & (ia >= 1) & (ia < FAR))
         def _():
@@ -240,11 +239,11 @@
             @pl.when(i == 0)
             def _():
                 q = mp(base, 0)
-                for k in range(NSUB):
+                for k in PIECES:
                     piece = ax.at[q, :, pl.ds(k * sub, sub)]
                     wait_bytes(piece, recv_sub.at[k])
                     if k >= NDIRECT:
-                        remote(piece, piece, send_first, recv_a.at[q], (x, z_out, t)).start()
+                        remote(piece, piece, send_pieces, recv_a.at[q], (x, z_out, t)).start()
                 pass_in(q)
 
             @pl.when((i >= 1) & (i < FAR))
@@ -468,14 +467,16 @@
     @pl.when(end)
     def _():
         wait_bytes(ax.at[pl.ds(0, FAR + NEAR)], send_ya)
+        wait_bytes(ax.at[0, :, pl.ds(0, NDIRECT * sub)], send_first)
         wait_bytes(ax.at[pl.ds(0, FAR)], send_zi)
 
     @pl.when(mid)
     def _():
-        wait_bytes(ax.at[pl.ds(0, FAR)], send_ya)
+        wait_bytes(ax.at[pl.ds(0, FAR - 1)], send_ya)
         wait_bytes(ax.at[pl.ds(0, 2 * FAR)], send_zi)
         wait_bytes(ax.at[pl.ds(0, 2 * FAR + NEAR - 1)], send_zo)
         wait_bytes(ax.at[0], send_first)
+        wait_bytes(ax.at[0, :, pl.ds(0, (NSUB - NDIRECT) * sub)], send_pieces)
 
     for k in range(1, 4):
         src = lax.rem(z + k, 4)
@@ -552,7 +553,7 @@
                 dma((NCH,)), dma, dma, dma, dma,
                 dma((NWC,)), dma((NWC,)), dma((NWC,)), dma, dma,
                 dma, dma, dma, dma,
-                dma((2, 3)), dma, dma((NHALF,)), dma((NSUB,)), dma,
+                dma((2, 3)), dma, dma((NHALF,)), dma((NSUB,)), dma, dma,
                 pltpu.SemaphoreType.REGULAR, pltpu.SemaphoreType.REGULAR,
                 dma((3,)), dma((4,)),
             ],

time: 252 us -> 253 us (level)
  no operation moved by 1% of the time
where the time goes in v7:
time: 253 us
  Pallas kernels  252 us (100%)
    pallas_call x1, Pallas kernels, local_step(): pl.pallas_call(kernel, out_shape=(pltpu.VMEM((rows, cols), f32), pltpu.VM...  246 us
    pallas_call x1, Pallas kernels, local_step(): pl.pallas_call(finish_kernel, out_shape=(jax.ShapeDtypeStruct((rows, cols...  6.08 us

profile of v7, /device:TPU:0, one launch (start us, length us, event | category | flops | bytes accessed | tf_op | source)
XLA Modules:
  0.0 253.0 jit_solution(18183018816828006801)
XLA Ops:
  0.6 0.0 copy-start
  0.6 246.3 %gather_project.1 = (f32[2048,2048]{1,0:T(8,128)S(1)}, f32[4,16,1,128]{3,2,1,0:T(1,128)S(1)}, bf16[64,2,32,2048]{3,2,1,0:T(8,128)(2,1)}, bf16[2048,2048]{1,0:T(8,128)(2,1)}) custom-call(bf16[8192,2048]{1,0:T(8,128)(2,1)} %a.1, bf16[2048,2048]{1,0:T(8,128)(2,1)} %w.1, bf16[2048,2048]{1,0:T(8,128)(2,1)} %r.1), custom_call_target="tpu_custom_call" | custom-call | tf_op jit(solution)/shard_map/gather_project/pallas_call | solution.py:537
  246.9 0.0 copy-done
  246.9 6.1 %norm_store.1 = (bf16[2048,2048]{1,0:T(8,128)(2,1)}, bf16[2048,2048]{1,0:T(8,128)(2,1)}) custom-call(f32[2048,2048]{1,0:T(8,128)S(1)} %get-tuple-element.4.h, f32[4,16,1,128]{3,2,1,0:T(1,128)S(1)} %get-tuple-element.5.ss, f32[1,2048]{1,0:T(1,128)S(1)} %bitcast.1), custom_call_target="tpu_custom_call" | custom-call | tf_op jit(solution)/shard_map/norm_store/pallas_call | solution.py:564
Async XLA Ops:
  0.6 246.3 %copy-start = (f32[2048]{0:T(1024)S(1)}, f32[2048]{0:T(1024)}, u32[]{:S(2)}) copy-start(f32[2048]{0:T(1024)} %param.7) | copy-start | bytes 24580

commit v8 on v7

--- a/solution.py
+++ b/solution.py
@@ -38,7 +38,7 @@
     return n
 
 
-END_UNITS = (19, 19, 20, 20, 21, 22, 24, 25, 28, 29, 32, 33, 36, 37, 39, 40)
+END_UNITS = (19, 19, 20, 20, 21, 22, 24, 25, 28, 29, 32, 33, 35, 36, 38, 40)
 MID_UNITS = (35, 35, 36, 36, 37, 37, 38, 38)
 
 
@@ -87,6 +87,9 @@
     def mp(start, j):
         return start + FAR + lax.rem(j + NEAR, FAR)
 
+    def private(m):
+        return base + FAR + jnp.where(m < NEAR // 2, m, NEAR // 2 + lax.rem(m + NEAR // 4, NEAR // 2))
+
     def chunk_rows(q):
         return pl.ds(pl.multiple_of(q * ch, ch), ch)
 
@@ -129,7 +132,8 @@
 
         @pl.when(end & (ia >= FAR) & (ia < FAR + NEAR))
         def _():
-            send_y_a(base + ia, wl.at[c, chunk_rows(base + ia)])
+            q = private(ia - FAR)
+            send_y_a(q, wl.at[c, chunk_rows(q)])
 
         @pl.when(mid & (ia == 0))
         def _():
@@ -152,6 +156,7 @@
     remote(a.at[prow], ap, send_da, recv_da, partner).start()
     own_w = pltpu.make_async_copy(w, wl.at[0], load_w)
     own_w.start()
+    ss_loc[...] = jnp.zeros_like(ss_loc)
 
     def load(q):
         here = pl.ds(pl.multiple_of(q * ch, ch), ch)
@@ -222,7 +227,7 @@
 
             @pl.when((i >= WS + FAR) & (i < WS + FAR + NEAR))
             def _():
-                arrive_late(base + i - WS)
+                arrive_late(private(i - WS - FAR))
 
             nlate = 1 + 2 * FAR + NEAR - LATE
 
@@ -336,12 +341,15 @@
     def unit_of(u):
         b = side * NUNIT
         o = (1 - side) * NUNIT
-        end_order = (b + 6, b + 7, o + 6, o + 7, b, o + 4, b + 1, o + 5, b + 2, o, b + 3, o + 1, b + 4, o + 2, b + 5, o + 3)
+        end_order = (b + 6, b + 7, o + 6, o + 7, b, o + 4, b + 1, o + 5, b + 2, o, b + 3, o + 1, b + 4, o + 2)
         mid_order = (b, b + 1, o, o + 1, b + 2, b + 3, o + 2, o + 3) + (0,) * NUNIT
-        q = jnp.int32(0)
-        for k in range(NHALF):
-            q = q + jnp.where(u == k, jnp.where(end, end_order[k], mid_order[k]), 0)
-        return q
+        both = []
+        for last in ((o + 3, b + 5), (b + 5, o + 3)):
+            q = jnp.int32(0)
+            for k in range(NHALF):
+                q = q + jnp.where(u == k, jnp.where(end, (end_order + last)[k], mid_order[k]), 0)
+            both.append(q)
+        return both
 
     def wait_load(q):
         here = pl.ds(pl.multiple_of(q * half, half), half)
@@ -361,22 +369,34 @@
             part = part + sq[:, k * 128:(k + 1) * 128]
         return part
 
-    def keep_squares(q, part):
-        ss_loc[q] = jnp.sum(part.T, axis=0, keepdims=True)
+    def keep_squares(q0, q1, part):
+        total = jnp.sum(part.T, axis=0, keepdims=True)
+        low = lax.broadcasted_iota(jnp.int32, total.shape, 1) < total.shape[1] // 2
+        ss_loc[q0] = jnp.where(low, total, ss_loc[q0])
+        ss_loc[q1] = jnp.where(low, ss_loc[q1], total)
 
     def remote_unit(u, _):
-        q = unit_of(u)
-        here = pl.ds(pl.multiple_of(q * half, half), half)
+        q0, q1 = unit_of(u)
+        quarter = half // 2
+        low = pl.ds(pl.multiple_of(q0 * half, quarter), quarter)
+        high = pl.ds(pl.multiple_of(q1 * half + quarter, quarter), quarter)
 
         @pl.when(mid | (u < NHALF - 4))
         def _():
-            wait_load(q)
+            wait_load(q0)
 
         def tile(n, part):
             cs = pl.ds(pl.multiple_of(n * tn, tn), tn)
-            return part + squares(far_product(here, cs))
-
-        keep_squares(q, lax.fori_loop(0, ntile, tile, jnp.zeros((half, 128), jnp.float32)))
+            far = [jnp.dot(jnp.concatenate([wl[b, low, :], wl[b, high, :]], axis=0), wr[b, :, cs],
+                           preferred_element_type=jnp.float32).astype(jnp.bfloat16).astype(jnp.float32) for b in range(2)]
+            far = far[0] + far[1]
+            v0 = acc[low, cs] + far[:quarter]
+            v1 = acc[high, cs] + far[quarter:]
+            acc[low, cs] = v0
+            acc[high, cs] = v1
+            return part + squares(jnp.concatenate([v0, v1], axis=0))
+
+        keep_squares(q0, q1, lax.fori_loop(0, ntile, tile, jnp.zeros((half, 128), jnp.float32)))
         return None
 
     def column_unit(k):
@@ -409,7 +429,7 @@
                 def tile(m, part):
                     return part + squares(acc[here, pl.ds(pl.multiple_of(m * tn, tn), tn)])
 
-                keep_squares(q, lax.fori_loop(0, ntile, tile, jnp.zeros((half, 128), jnp.float32)))
+                keep_squares(q, q, lax.fori_loop(0, ntile, tile, jnp.zeros((half, 128), jnp.float32)))
                 return None
 
             lax.fori_loop(0, 8, sums, None)

time: 253 us -> 254 us (level)
  no operation moved by 1% of the time
where the time goes in v8:
time: 254 us
  Pallas kernels  253 us (100%)
    pallas_call x1, Pallas kernels, local_step(): pl.pallas_call(kernel, out_shape=(pltpu.VMEM((rows, cols), f32), pltpu.VM...  247 us
    pallas_call x1, Pallas kernels, local_step(): pl.pallas_call(finish_kernel, out_shape=(jax.ShapeDtypeStruct((rows, cols...  6.08 us

profile of v8, /device:TPU:0, one launch (start us, length us, event | category | flops | bytes accessed | tf_op | source)
XLA Modules:
  0.0 253.7 jit_solution(6546487460687940562)
XLA Ops:
  0.6 0.0 copy-start
  0.6 247.0 %gather_project.1 = (f32[2048,2048]{1,0:T(8,128)S(1)}, f32[4,16,1,128]{3,2,1,0:T(1,128)S(1)}, bf16[64,2,32,2048]{3,2,1,0:T(8,128)(2,1)}, bf16[2048,2048]{1,0:T(8,128)(2,1)}) custom-call(bf16[8192,2048]{1,0:T(8,128)(2,1)} %a.1, bf16[2048,2048]{1,0:T(8,128)(2,1)} %w.1, bf16[2048,2048]{1,0:T(8,128)(2,1)} %r.1), custom_call_target="tpu_custom_call" | custom-call | tf_op jit(solution)/shard_map/gather_project/pallas_call | solution.py:557
  247.6 0.0 copy-done
  247.6 6.1 %norm_store.1 = (bf16[2048,2048]{1,0:T(8,128)(2,1)}, bf16[2048,2048]{1,0:T(8,128)(2,1)}) custom-call(f32[2048,2048]{1,0:T(8,128)S(1)} %get-tuple-element.4.h, f32[4,16,1,128]{3,2,1,0:T(1,128)S(1)} %get-tuple-element.5.ss, f32[1,2048]{1,0:T(1,128)S(1)} %bitcast.1), custom_call_target="tpu_custom_call" | custom-call | tf_op jit(solution)/shard_map/norm_store/pallas_call | solution.py:584
Async XLA Ops:
  0.6 247.0 %copy-start = (f32[2048]{0:T(1024)S(1)}, f32[2048]{0:T(1024)}, u32[]{:S(2)}) copy-start(f32[2048]{0:T(1024)} %param.7) | copy-start | bytes 24580

commit v9 on v6

--- a/solution.py
+++ b/solution.py
@@ -21,6 +21,7 @@
 LATE = FAR // 2
 NBUF = 4
 NDIRECT = 2
+LAG = 6
 NSUB = 4
 AHEAD = 12
 NSLOT = 2 * FAR + NEAR + 1
@@ -37,7 +38,7 @@
     return n
 
 
-END_UNITS = (19, 19, 20, 20, 21, 22, 24, 25, 28, 29, 32, 33, 36, 37, 39, 40)
+END_UNITS = (20, 20, 21, 22, 23, 24, 26, 28, 30, 31, 32, 33, 36, 37, 39, 40)
 MID_UNITS = (35, 35, 36, 36, 37, 37, 38, 38)
 
 
@@ -148,9 +149,22 @@
 
     lax.fori_loop(0, AHEAD, lambda i, _: (y_sends(i), None)[1], None)
 
-    remote(w, wl.at[1], send_dw, recv_dw, partner).start()
-    prow = pl.ds(pl.multiple_of((y * 2 + 1 - c) * rows, rows), rows)
-    remote(a.at[prow], ap, send_da, recv_da, partner).start()
+    kpart = kb // NUNIT
+
+    def partner_sends(i):
+        @pl.when(i < NUNIT // 2)
+        def _():
+            for k in range(2):
+                rs = pl.ds(pl.multiple_of((2 * i + k) * kpart, kpart), kpart)
+                remote(w.at[rs], wl.at[1, rs], send_dw, recv_dw, partner).start()
+
+        u = i - NUNIT // 2
+
+        @pl.when((u >= 0) & (u < NUNIT))
+        def _():
+            src = pl.ds(pl.multiple_of((y * 2 + 1 - c) * rows + u * unit, unit), unit)
+            remote(a.at[src], ap.at[pl.ds(pl.multiple_of(u * unit, unit), unit)], send_da, recv_da.at[u], partner).start()
+
     own_w = pltpu.make_async_copy(w, wl.at[0], load_w)
     own_w.start()
 
@@ -227,9 +241,13 @@
 
             nlate = 1 + 2 * FAR + NEAR - LATE
 
-            @pl.when((i >= 1) & (i < nlate))
-            def _():
-                arrive(z_chunk(i - 1), i)
+            @pl.when((i >= 1 + LAG) & (i < nlate - 1))
+            def _():
+                arrive(z_chunk(i - 1 - LAG), i)
+
+            @pl.when(i == nlate - 1)
+            def _():
+                lax.fori_loop(nlate - 2 - LAG, nlate - 1, lambda j, _: (arrive(z_chunk(j), i), None)[1], None)
 
             @pl.when((i >= nlate) & (i < nlate + LATE))
             def _():
@@ -292,7 +310,7 @@
             load(jnp.where(end, z_chunk(j), mp(other, j)))
             return None
 
-        lax.fori_loop(0, LOADS - 1, from_z, None)
+        lax.fori_loop(0, jnp.where(end, LOADS - 1 - LAG, LOADS - 1), from_z, None)
 
         def from_y(j, _):
             load(mp(base, j))
@@ -319,6 +337,7 @@
 
         @pl.when(u + 1 < NUNIT)
         def _():
+            wait_bytes(ap.at[pl.ds(pl.multiple_of((u + 1) * unit, unit), unit)], recv_da.at[u + 1])
             for cp in local_loads(u + 1):
                 cp.start()
 
@@ -337,7 +356,7 @@
     def unit_of(u):
         b = side * NUNIT
         o = (1 - side) * NUNIT
-        end_order = (b + 6, b + 7, o + 6, o + 7, b, o + 4, b + 1, o + 5, b + 2, o, b + 3, o + 1, b + 4, o + 2, b + 5, o + 3)
+        end_order = (b + 6, b + 7, o + 6, o + 7, b, b + 1, o + 4, b + 2, o + 5, b + 3, o, o + 1, b + 4, o + 2, b + 5, o + 3)
         mid_order = (b, b + 1, o, o + 1, b + 2, b + 3, o + 2, o + 3) + (0,) * NUNIT
         q = jnp.int32(0)
         for k in range(NHALF):
@@ -416,6 +435,8 @@
             lax.fori_loop(0, 8, sums, None)
 
     def slot_body(i, _):
+        partner_sends(i)
+
         @pl.when(i == LOADS)
         def _():
             early_loads()
@@ -432,7 +453,7 @@
         def _():
             own_w.wait()
             wait_bytes(wl.at[1], recv_dw)
-            wait_bytes(ap, recv_da)
+            wait_bytes(ap.at[pl.ds(0, unit)], recv_da.at[0])
             for cp in local_loads(0):
                 cp.start()
 
@@ -551,7 +572,7 @@
                 pltpu.VMEM((NHALF, 1, 128), f32),
                 dma((NCH,)), dma, dma, dma, dma,
                 dma((NWC,)), dma((NWC,)), dma((NWC,)), dma, dma,
-                dma, dma, dma, dma,
+                dma((NUNIT,)), dma, dma, dma,
                 dma((2, 3)), dma, dma((NHALF,)), dma((NSUB,)), dma,
                 pltpu.SemaphoreType.REGULAR, pltpu.SemaphoreType.REGULAR,
                 dma((3,)), dma((4,)),

time: 252 us -> 252 us (level)
  no operation moved by 1% of the time
where the time goes in v9:
time: 252 us; the launch traced here: 251 us
  Pallas kernels  251 us (100%)
    pallas_call x1, Pallas kernels, local_step(): pl.pallas_call(kernel, out_shape=(pltpu.VMEM((rows, cols), f32), pltpu.VM...  245 us
    pallas_call x1, Pallas kernels, local_step(): pl.pallas_call(finish_kernel, out_shape=(jax.ShapeDtypeStruct((rows, cols...  6.08 us

profile of v9, /device:TPU:0, one launch (start us, length us, event | category | flops | bytes accessed | tf_op | source)
XLA Modules:
  0.0 251.4 jit_solution(18435341870702665454)
XLA Ops:
  0.6 0.0 copy-start
  0.6 244.6 %gather_project.1 = (f32[2048,2048]{1,0:T(8,128)S(1)}, f32[4,16,1,128]{3,2,1,0:T(1,128)S(1)}, bf16[64,2,32,2048]{3,2,1,0:T(8,128)(2,1)}, bf16[2048,2048]{1,0:T(8,128)(2,1)}) custom-call(bf16[8192,2048]{1,0:T(8,128)(2,1)} %a.1, bf16[2048,2048]{1,0:T(8,128)(2,1)} %w.1, bf16[2048,2048]{1,0:T(8,128)(2,1)} %r.1), custom_call_target="tpu_custom_call" | custom-call | tf_op jit(solution)/shard_map/gather_project/pallas_call | solution.py:557
  245.3 0.0 copy-done
  245.3 6.1 %norm_store.1 = (bf16[2048,2048]{1,0:T(8,128)(2,1)}, bf16[2048,2048]{1,0:T(8,128)(2,1)}) custom-call(f32[2048,2048]{1,0:T(8,128)S(1)} %get-tuple-element.4.h, f32[4,16,1,128]{3,2,1,0:T(1,128)S(1)} %get-tuple-element.5.ss, f32[1,2048]{1,0:T(1,128)S(1)} %bitcast.1), custom_call_target="tpu_custom_call" | custom-call | tf_op jit(solution)/shard_map/norm_store/pallas_call | solution.py:584
Async XLA Ops:
  0.6 244.6 %copy-start = (f32[2048]{0:T(1024)S(1)}, f32[2048]{0:T(1024)}, u32[]{:S(2)}) copy-start(f32[2048]{0:T(1024)} %param.7) | copy-start | bytes 24580

commit v10 on v9

--- a/solution.py
+++ b/solution.py
@@ -20,7 +20,6 @@
 HGRP = NCH // NHALF
 LATE = FAR // 2
 NBUF = 4
-NDIRECT = 2
 LAG = 6
 NSUB = 4
 AHEAD = 12
@@ -82,10 +81,7 @@
         pl.semaphore_signal(barrier, inc=1, device_id=dev, device_id_type=MESH)
     for k in range(1, 4):
         pl.semaphore_signal(barrier, inc=1, device_id=(x, lax.rem(z + k, 4), t), device_id_type=MESH)
-    z_mate = jnp.where(end, z_in, z_out)
-    for cc in range(2):
-        pl.semaphore_signal(barrier, inc=1, device_id=(x, z_mate, (1 - y) * 2 + cc), device_id_type=MESH)
-    pl.semaphore_wait(barrier, 9)
+    pl.semaphore_wait(barrier, 7)
 
     def mp(start, j):
         return start + FAR + lax.rem(j + NEAR, FAR)
@@ -101,11 +97,6 @@
                    (x, z, (1 - y) * 2 + cc)).start()
 
     def send_y_first(q):
-        for k in range(NDIRECT):
-            for cc in range(2):
-                row = ((1 - y) * 2 + cc) * rows + q * ch + k * sub
-                remote(a.at[pl.ds(pl.multiple_of(row, sub), sub)], ax.at[q, c, pl.ds(k * sub, sub)], send_first,
-                       recv_a.at[q], (x, z_out, (1 - y) * 2 + cc)).start()
         for k in range(NSUB):
             for cc in range(2):
                 row = ((1 - y) * 2 + cc) * rows + q * ch + k * sub
@@ -261,8 +252,7 @@
                 for k in range(NSUB):
                     piece = ax.at[q, :, pl.ds(k * sub, sub)]
                     wait_bytes(piece, recv_sub.at[k])
-                    if k >= NDIRECT:
-                        remote(piece, piece, send_first, recv_a.at[q], (x, z_out, t)).start()
+                    remote(piece, piece, send_first, recv_a.at[q], (x, z_out, t)).start()
                 pass_in(q)
 
             @pl.when((i >= 1) & (i < FAR))

time: 252 us -> 252 us (level)
  no operation moved by 1% of the time
where the time goes in v10:
time: 252 us; the launch traced here: 251 us
  Pallas kernels  251 us (100%)
    pallas_call x1, Pallas kernels, local_step(): pl.pallas_call(kernel, out_shape=(pltpu.VMEM((rows, cols), f32), pltpu.VM...  245 us
    pallas_call x1, Pallas kernels, local_step(): pl.pallas_call(finish_kernel, out_shape=(jax.ShapeDtypeStruct((rows, cols...  6.08 us

profile of v10, /device:TPU:0, one launch (start us, length us, event | category | flops | bytes accessed | tf_op | source)
XLA Modules:
  0.0 251.4 jit_solution(5051682976204823910)
XLA Ops:
  0.6 0.0 copy-start
  0.6 244.7 %gather_project.1 = (f32[2048,2048]{1,0:T(8,128)S(1)}, f32[4,16,1,128]{3,2,1,0:T(1,128)S(1)}, bf16[64,2,32,2048]{3,2,1,0:T(8,128)(2,1)}, bf16[2048,2048]{1,0:T(8,128)(2,1)}) custom-call(bf16[8192,2048]{1,0:T(8,128)(2,1)} %a.1, bf16[2048,2048]{1,0:T(8,128)(2,1)} %w.1, bf16[2048,2048]{1,0:T(8,128)(2,1)} %r.1), custom_call_target="tpu_custom_call" | custom-call | tf_op jit(solution)/shard_map/gather_project/pallas_call | solution.py:547
  245.3 0.0 copy-done
  245.4 6.1 %norm_store.1 = (bf16[2048,2048]{1,0:T(8,128)(2,1)}, bf16[2048,2048]{1,0:T(8,128)(2,1)}) custom-call(f32[2048,2048]{1,0:T(8,128)S(1)} %get-tuple-element.4.h, f32[4,16,1,128]{3,2,1,0:T(1,128)S(1)} %get-tuple-element.5.ss, f32[1,2048]{1,0:T(1,128)S(1)} %bitcast.1), custom_call_target="tpu_custom_call" | custom-call | tf_op jit(solution)/shard_map/norm_store/pallas_call | solution.py:574
Async XLA Ops:
  0.6 244.7 %copy-start = (f32[2048]{0:T(1024)S(1)}, f32[2048]{0:T(1024)}, u32[]{:S(2)}) copy-start(f32[2048]{0:T(1024)} %param.7) | copy-start | bytes 24580

commit v11 on v10

--- a/solution.py
+++ b/solution.py
@@ -468,6 +468,7 @@
 
     lax.fori_loop(0, NSLOT, slot_body, None)
 
+    ss_all[z] = ss_loc[...]
     for k in range(1, 4):
         remote(ss_loc, ss_all.at[z], send_ss.at[k - 1], recv_ss.at[z], (x, lax.rem(z + k, 4), t)).start()
     wait_bytes(wl.at[1], send_dw)
@@ -492,7 +493,6 @@
         src = lax.rem(z + k, 4)
         remote(ss_loc, ss_all.at[src], send_ss.at[k - 1], recv_ss.at[src], (x, src, t)).wait_recv()
         remote(ss_loc, ss_all.at[src], send_ss.at[k - 1], recv_ss.at[src], (x, src, t)).wait_send()
-    ss_all[z] = ss_loc[...]
 
 def finish_kernel(h, ss, g, h_out, n_out, hbuf, nbuf, sem):
     rows, cols = h.shape

time: 252 us -> 252 us (level)
  no operation moved by 1% of the time
where the time goes in v11:
time: 252 us; the launch traced here: 251 us
  Pallas kernels  251 us (100%)
    pallas_call x1, Pallas kernels, local_step(): pl.pallas_call(kernel, out_shape=(pltpu.VMEM((rows, cols), f32), pltpu.VM...  245 us
    pallas_call x1, Pallas kernels, local_step(): pl.pallas_call(finish_kernel, out_shape=(jax.ShapeDtypeStruct((rows, cols...  6.08 us

profile of v11, /device:TPU:0, one launch (start us, length us, event | category | flops | bytes accessed | tf_op | source)
XLA Modules:
  0.0 251.5 jit_solution(2817073525502969558)
XLA Ops:
  0.6 0.0 copy-start
  0.6 244.7 %gather_project.1 = (f32[2048,2048]{1,0:T(8,128)S(1)}, f32[4,16,1,128]{3,2,1,0:T(1,128)S(1)}, bf16[64,2,32,2048]{3,2,1,0:T(8,128)(2,1)}, bf16[2048,2048]{1,0:T(8,128)(2,1)}) custom-call(bf16[8192,2048]{1,0:T(8,128)(2,1)} %a.1, bf16[2048,2048]{1,0:T(8,128)(2,1)} %w.1, bf16[2048,2048]{1,0:T(8,128)(2,1)} %r.1), custom_call_target="tpu_custom_call" | custom-call | tf_op jit(solution)/shard_map/gather_project/pallas_call | solution.py:547
  245.4 0.0 copy-done
  245.4 6.1 %norm_store.1 = (bf16[2048,2048]{1,0:T(8,128)(2,1)}, bf16[2048,2048]{1,0:T(8,128)(2,1)}) custom-call(f32[2048,2048]{1,0:T(8,128)S(1)} %get-tuple-element.4.h, f32[4,16,1,128]{3,2,1,0:T(1,128)S(1)} %get-tuple-element.5.ss, f32[1,2048]{1,0:T(1,128)S(1)} %bitcast.1), custom_call_target="tpu_custom_call" | custom-call | tf_op jit(solution)/shard_map/norm_store/pallas_call | solution.py:574
Async XLA Ops:
  0.6 244.7 %copy-start = (f32[2048]{0:T(1024)S(1)}, f32[2048]{0:T(1024)}, u32[]{:S(2)}) copy-start(f32[2048]{0:T(1024)} %param.7) | copy-start | bytes 24580
